TPU v7x, 32 devices: a whole 2x2x4 slice. The times are simulated.
32 devices in a mesh: dp: 2 (over x), expert: 16 (over z, y, core).
Axes of the slice: x: 2, y: 2, z: 4, core: 2. Of those that a mesh axis runs over, the one named last changes fastest.
Arguments:
- tokens: bfloat16 [512, 2048], P('expert', 'dp'), may hold values from -6 to 6
- routes: int32 [512, 8], P('expert'), may hold values from 0 to 63, all different within a row; in each aligned block of 32 rows (0 to 31, 32 to 63, ...) at most 4 rows name the same one
- route_weight: float32 [512, 8], P('expert'), may hold values from 0.05 to 0.5
- gate_weight: bfloat16 [64, 2048, 768], P('expert', 'dp'), may hold values from -0.125 to 0.125
- up_weight: bfloat16 [64, 2048, 768], P('expert', 'dp'), may hold values from -0.125 to 0.125
- down_weight: bfloat16 [64, 768, 2048], P('expert', None, 'dp'), may hold values from -0.21875 to 0.21875
- trained_down: float32 [64, 768, 2048], P('expert', 'dp'), may hold values from -0.21875 to 0.21875
Outputs:
- mixed: bfloat16 [512, 2048], P('expert', 'dp')
- synced_down: bfloat16 [64, 768, 2048], P('expert', None, 'dp')
Inputs may be any that keep to these rules, and one draw needn't show every extreme that they name: `routes`: each row names 8 different experts. Among the 32 rows of one device (aligned blocks), no expert is named more than 4 times, a bound that some block reaches.
All inputs are finite; a program needn't handle non-finite values.
Results may differ from a plain program's by a relative error of at most 0.0058.
Values may be sent and summed in bfloat16 or wider, within the bound.
No kernel may reach another device: no remote copies, remote signals or barrier semaphores. Data moves between devices by JAX's collectives and lax.ppermute only.
A program may use at most 128 MiB of HBM per device.

v0:
```python
import jax
import jax.numpy as jnp
from jax import lax
from jax.sharding import PartitionSpec as P

CAP = 4


def local(tokens, routes, route_weight, gate_weight, up_weight, down_weight, trained_down):
    tok_rows, width_local = tokens.shape
    expert_local = gate_weight.shape[0]
    groups = lax.axis_size("expert")
    experts_all = expert_local * groups
    capacity = CAP
    narrowed = trained_down.astype(jnp.bfloat16)
    synced_down = lax.all_to_all(narrowed, "dp", split_axis=2, concat_axis=1, tiled=True)
    labels = lax.broadcasted_iota(jnp.int32, (1, 1, experts_all), 2)
    chosen = routes[:, :, None] == labels
    counts = jnp.sum(chosen.astype(jnp.int32), axis=1)
    earlier = jnp.cumsum(counts, axis=0) - counts
    weight_expert = jnp.sum(jnp.where(chosen, route_weight[:, :, None], 0.0), axis=1)
    slot_ids = lax.broadcasted_iota(jnp.int32, (1, 1, capacity), 2)
    placed = (counts[:, :, None] == 1) & (earlier[:, :, None] == slot_ids)
    dispatch = placed.astype(jnp.bfloat16).reshape(tok_rows, experts_all * capacity)
    outgoing = jnp.dot(dispatch.T, tokens, preferred_element_type=jnp.float32).astype(jnp.bfloat16)
    outgoing = outgoing.reshape(groups, expert_local, capacity, width_local)
    arrived = lax.all_to_all(outgoing, "expert", split_axis=0, concat_axis=2, tiled=True)
    arrived = arrived.reshape(expert_local, groups * capacity, width_local)
    gate_part = jnp.einsum("erd,edf->erf", arrived, gate_weight, preferred_element_type=jnp.float32)
    up_part = jnp.einsum("erd,edf->erf", arrived, up_weight, preferred_element_type=jnp.float32)
    gate_sum, up_sum = lax.psum((gate_part, up_part), "dp")
    hidden = (jax.nn.silu(gate_sum) * up_sum).astype(jnp.bfloat16)
    expert_out = jnp.einsum("erf,efd->erd", hidden, down_weight, preferred_element_type=jnp.float32)
    expert_out = expert_out.astype(jnp.bfloat16).reshape(
        1, expert_local, groups * capacity, width_local
    )
    returned = lax.all_to_all(expert_out, "expert", split_axis=2, concat_axis=0, tiled=True)
    returned = returned.reshape(experts_all * capacity, width_local)
    combine = (weight_expert[:, :, None] * placed.astype(jnp.float32)).reshape(
        tok_rows, experts_all * capacity
    )
    mixed = jnp.dot(
        combine,
        returned.astype(jnp.float32),
        precision=lax.Precision.HIGHEST,
        preferred_element_type=jnp.float32,
    )
    mixed = mixed.astype(jnp.bfloat16)
    return (mixed, synced_down)


def solution(mesh):
    placed = (
        P("expert", "dp"),
        P("expert", None),
        P("expert", None),
        P("expert", "dp", None),
        P("expert", "dp", None),
        P("expert", None, "dp"),
        P("expert", "dp", None),
    )
    return jax.shard_map(
        local,
        mesh=mesh,
        in_specs=placed,
        out_specs=(P("expert", "dp"), P("expert", None, "dp")),
        check_vma=False,
    )
```

profile of v0, /device:TPU:0, one launch (start us, length us, event | category | flops | bytes accessed | tf_op | source)
XLA Modules:
  0.0 169.0 jit_solution(15990197071940273313)
XLA Ops:
  7.2 0.0 copy-start
  7.2 0.8 copy.29
  8.0 0.1 convert_reduce_fusion
  8.1 0.1 copy.30
  8.2 0.1 reduce_window_sum.11
  8.3 0.1 copy.31
  8.4 0.1 eq.66
  8.5 0.0 copy-done
  8.6 0.3 convolution_convert_fusion.1
  8.9 1.0 reshape.79
  9.9 7.4 %all-to-all-start = ((bf16[16,4,4,1024]{3,2,1,0:T(4,128)(2,1)}), bf16[16,4,4,1024]{3,2,1,0:T(4,128)(2,1)S(1)}, u32[]{:S(2)}, u32[]{:S(2)}) async-start(bf16[16,4,4,1024]{3,2,1,0:T(4,128)(2,1)} %reshape.79), calls=%async_computation | async-start | bytes 1048576 | tf_op jit(solution)/shard_map/all_to_all | solution.py:27
  17.3 12.5 %copy.37 = bf16[4,384,2048]{1,0,2:T(4,128)(2,1)} copy(f32[4,384,2048]{2,1,0:T(8,128)} %param.13) | data formatting | bytes 18874368 | tf_op args[6]
  29.8 1.7 %all-to-all-done = bf16[16,4,4,1024]{3,2,1,0:T(4,128)(2,1)S(1)} async-done(((bf16[16,4,4,1024]{3,2,1,0:T(4,128)(2,1)}), bf16[16,4,4,1024]{3,2,1,0:T(4,128)(2,1)S(1)}, u32[]{:S(2)}, u32[]{:S(2)}) %all-to-all-start) | async-done | bytes 524320 | tf_op jit(solution)/shard_map/all_to_all | solution.py:27
  31.6 6.3 %all-to-all-start.2 = ((bf16[4,384,2048]{1,0,2:T(4,128)(2,1)}), bf16[4,384,2048]{1,0,2:T(4,128)(2,1)}, u32[]{:S(2)}, u32[]{:S(2)}) async-start(bf16[4,384,2048]{1,0,2:T(4,128)(2,1)} %copy.37), calls=%async_computation.2 | async-start | bytes 12582912 | tf_op jit(solution)/shard_map/all_to_all | solution.py:16
  37.9 0.0 all-reduce.3.cloned.1.call-start
  37.9 0.2 copy.34
  38.1 0.1 reshape.80
  38.3 4.9 %fusion.9 = f32[4,64,768]{2,1,0:T(8,128)} fusion(bf16[4,64,1024]{2,1,0:T(8,128)(2,1)S(1)} %reshape.80, bf16[4,1024,768]{2,1,0:T(8,128)(2,1)} %param.11), kind=kOutput, calls=%fused_computation.19 | convolution fusion | flops 402653184 | bytes 7602176 | tf_op jit(solution)/shard_map/erd,edf->erf/dot_general | solution.py:30
  43.2 4.9 %fusion.8 = f32[4,64,768]{2,1,0:T(8,128)} fusion(bf16[4,64,1024]{2,1,0:T(8,128)(2,1)S(1)} %reshape.80, bf16[4,1024,768]{2,1,0:T(8,128)(2,1)} %param.10), kind=kOutput, calls=%fused_computation.18 | convolution fusion | flops 402653184 | bytes 7602176 | tf_op jit(solution)/shard_map/erd,edf->erf/dot_general | solution.py:29
  48.1 0.0 all-reduce.3.cloned.1.call-update
  48.1 85.6 %all-reduce.3.cloned.1.call-done = (f32[4,64,768]{2,1,0:T(8,128)}, f32[4,64,768]{2,1,0:T(8,128)}) async-done(((f32[4,64,768]{2,1,0:T(8,128)}, f32[4,64,768]{2,1,0:T(8,128)}), (f32[4,64,768]{2,1,0:T(8,128)}, f32[4,64,768]{2,1,0:T(8,128)})) %all-reduce.3.cloned.1.call-update) | async-done | bytes 1572880 | tf_op jit(solution)/shard_map/psum | solution.py:31
  133.7 0.0 copy-start.1
  133.7 4.5 %fusion = bf16[1,4,64,1024]{3,2,1,0:T(8,128)(2,1)S(1)} fusion(bf16[4,768,1024]{2,1,0:T(8,128)(2,1)} %param.12, f32[4,64,768]{2,1,0:T(8,128)} %get-tuple-element.2, f32[4,64,768]{2,1,0:T(8,128)} %get-tuple-element.3), kind=kOutput, calls=%fused_computation.2 | convolution fusion | flops 404094976 | bytes 8388608 | tf_op jit(solution)/shard_map/erf,efd->erd/dot_general | solution.py:33
  138.2 1.2 copy.35
  139.4 2.6 %all-to-all-done.2 = bf16[4,384,2048]{1,0,2:T(4,128)(2,1)} async-done(((bf16[4,384,2048]{1,0,2:T(4,128)(2,1)}), bf16[4,384,2048]{1,0,2:T(4,128)(2,1)}, u32[]{:S(2)}, u32[]{:S(2)}) %all-to-all-start.2) | async-done | bytes 6291488 | tf_op jit(solution)/shard_map/all_to_all | solution.py:16
  142.0 4.4 %all-to-all-start.1 = ((bf16[1,4,64,1024]{3,1,0,2:T(4,128)(2,1)}), bf16[1,4,64,1024]{3,1,0,2:T(4,128)(2,1)S(1)}, u32[]{:S(2)}, u32[]{:S(2)}) async-start(bf16[1,4,64,1024]{3,1,0,2:T(4,128)(2,1)} %copy.35), calls=%async_computation.1 | async-start | bytes 1048576 | tf_op jit(solution)/shard_map/all_to_all | solution.py:37
  146.4 0.0 copy-done.1
  146.5 0.1 copy.32
  146.5 0.1 select_reduce_fusion
  146.7 0.1 copy.33
  146.8 0.1 fusion.3
  146.8 10.5 %copy.38 = bf16[4,2,384,1024]{3,2,1,0:T(8,128)(2,1)} copy(bf16[4,2,384,1024]{2,0,3,1:T(4,128)(2,1)} %bitcast.9) | data formatting | bytes 12582912 | tf_op jit(solution)/shard_map/all_to_all | solution.py:16
  157.4 3.3 %all-to-all-done.1 = bf16[1,4,64,1024]{3,1,0,2:T(4,128)(2,1)S(1)} async-done(((bf16[1,4,64,1024]{3,1,0,2:T(4,128)(2,1)}), bf16[1,4,64,1024]{3,1,0,2:T(4,128)(2,1)S(1)}, u32[]{:S(2)}, u32[]{:S(2)}) %all-to-all-start.1) | async-done | bytes 524320 | tf_op jit(solution)/shard_map/all_to_all | solution.py:37
  160.7 0.3 copy.40
  161.0 0.1 reshape.82
  161.1 1.0 convolution_convert_fusion.2
  (5 shorter events, 0.1 us)
Async XLA Ops:
  7.2 1.4 copy-start
  9.9 21.7 %all-to-all-start = ((bf16[16,4,4,1024]{3,2,1,0:T(4,128)(2,1)}), bf16[16,4,4,1024]{3,2,1,0:T(4,128)(2,1)S(1)}, u32[]{:S(2)}, u32[]{:S(2)}) async-start(bf16[16,4,4,1024]{3,2,1,0:T(4,128)(2,1)} %reshape.79), calls=%async_computation | async-start | bytes 1048576 | tf_op jit(solution)/shard_map/all_to_all | solution.py:27
  31.6 110.4 %all-to-all-start.2 = ((bf16[4,384,2048]{1,0,2:T(4,128)(2,1)}), bf16[4,384,2048]{1,0,2:T(4,128)(2,1)}, u32[]{:S(2)}, u32[]{:S(2)}) async-start(bf16[4,384,2048]{1,0,2:T(4,128)(2,1)} %copy.37), calls=%async_computation.2 | async-start | bytes 12582912 | tf_op jit(solution)/shard_map/all_to_all | solution.py:16
  37.9 95.8 %all-reduce.3.cloned.1.call-start = ((), (), s32[]{:S(2)}) async-start(), calls=%async_computation.3 | async-start | bytes 3145728 | tf_op jit(solution)/shard_map/psum | solution.py:31
  133.7 12.7 %copy-start.1 = (f32[32,8]{0,1:T(8,128)S(1)}, f32[32,8]{0,1:T(8,128)}, u32[]{:S(2)}) copy-start(f32[32,8]{0,1:T(8,128)} %param.9) | copy-start | bytes 3076
  142.0 18.7 %all-to-all-start.1 = ((bf16[1,4,64,1024]{3,1,0,2:T(4,128)(2,1)}), bf16[1,4,64,1024]{3,1,0,2:T(4,128)(2,1)S(1)}, u32[]{:S(2)}, u32[]{:S(2)}) async-start(bf16[1,4,64,1024]{3,1,0,2:T(4,128)(2,1)} %copy.35), calls=%async_computation.1 | async-start | bytes 1048576 | tf_op jit(solution)/shard_map/all_to_all | solution.py:37
Sparse Core Ops, SparseCore 0:
  48.2 85.4 all-reduce.2
where the time goes:
time: 170 us; the launch traced here: 169 us
  waiting for transfers between devices  93.3 us (55%)
  local copies, waits for them, and re-layouts  27.3 us (16%)
  starting transfers between devices  18.2 us (11%)
  matrix products  15.7 us (9%)
  between operations  14.2 us (8%)
    psum x1, waiting for transfers between devices, local(): gate_sum, up_sum = lax.psum((gate_part, up_part), 'dp')  85.6 us
    unnamed x7, local copies, waits for them, and re-layouts  13.4 us
    all_to_all x1, local copies, waits for them, and re-layouts, local(): lax.all_to_all(narrowed, 'dp', split_axis=2, concat_axis=1, tiled=True)  10.5 us
    all_to_all x1, starting transfers between devices, local(): lax.all_to_all(outgoing, 'expert', split_axis=0, concat_axis=2, tiled=True)  7.41 us
    all_to_all x1, starting transfers between devices, local(): lax.all_to_all(narrowed, 'dp', split_axis=2, concat_axis=1, tiled=True)  6.29 us
    dot_general x1, matrix products, local(): jnp.einsum('erd,edf->erf', arrived, gate_weight, preferred_element_type=j...  4.91 us
    dot_general x1, matrix products, local(): jnp.einsum('erd,edf->erf', arrived, up_weight, preferred_element_type=jnp...  4.9 us
    dot_general x1, matrix products, local(): jnp.einsum('erf,efd->erd', hidden, down_weight, preferred_element_type=jn...  4.5 us
  transfers between devices with their start and end apart: 4, of which 4 were waited for; matrix products, arithmetic and copies ran while one was open for 23% of the time, Pallas kernels for 0%

commit v1 on v0

v1 whole, which is shorter than its diff:
```python
import jax
import jax.numpy as jnp
from jax import lax
from jax.sharding import PartitionSpec as P


CAP = 4
PIECES = 2


def ring(size, shift):
    return [(i, (i + shift) % size) for i in range(size)]


def local(tokens, routes, route_weight, gate_weight, up_weight, down_weight, trained_down):
    tok_rows, width_local = tokens.shape
    expert_local, hid, _ = down_weight.shape
    trained_rows = trained_down.shape[1]
    groups = lax.axis_size("expert")
    ways = lax.axis_size("dp")
    me = lax.axis_index("dp")
    experts_all = expert_local * groups
    capacity = CAP
    rows = groups * capacity
    share = rows // ways
    piece = trained_rows // PIECES

    def columns(source, expert, part, owner):
        strip = source[expert, part * piece:(part + 1) * piece]
        if ways == 2:
            strip = jnp.where(owner == 0, strip[:, :width_local], strip[:, width_local:])
        else:
            strip = lax.dynamic_slice_in_dim(strip, owner * width_local, width_local, 1)
        return strip.astype(jnp.bfloat16)

    arrivals = {}
    order = [(e, p) for e in range(expert_local) for p in range(PIECES)]
    for expert, part in order:
        arrivals[expert, part] = [
            lax.ppermute(columns(trained_down, expert, part, (me + s) % ways), "dp", ring(ways, s))
            for s in range(1, ways)
        ]

    labels = lax.broadcasted_iota(jnp.int32, (1, 1, experts_all), 2)
    chosen = routes[:, :, None] == labels
    counts = jnp.sum(chosen.astype(jnp.int32), axis=1)
    earlier = jnp.cumsum(counts, axis=0) - counts
    weight_expert = jnp.sum(jnp.where(chosen, route_weight[:, :, None], 0.0), axis=1)
    slot_ids = lax.broadcasted_iota(jnp.int32, (1, 1, capacity), 2)
    placed = (counts[:, :, None] == 1) & (earlier[:, :, None] == slot_ids)
    dispatch = placed.astype(jnp.bfloat16).reshape(tok_rows, experts_all * capacity)
    outgoing = jnp.dot(dispatch.T, tokens, preferred_element_type=jnp.float32).astype(jnp.bfloat16)
    own_source, outgoing = lax.optimization_barrier((trained_down, outgoing))
    outgoing = outgoing.reshape(groups, expert_local, capacity, width_local)
    arrived = lax.all_to_all(outgoing, "expert", split_axis=0, concat_axis=2, tiled=True)
    arrived = arrived.reshape(expert_local, rows, width_local)

    gate_part = jnp.einsum("erd,edf->erf", arrived, gate_weight, preferred_element_type=jnp.float32)
    up_part = jnp.einsum("erd,edf->erf", arrived, up_weight, preferred_element_type=jnp.float32)
    gate_part = gate_part.reshape(expert_local, ways, share, hid)
    up_part = up_part.reshape(expert_local, ways, share, hid)

    def share_of(array, owner):
        return lax.dynamic_index_in_dim(array, owner, 1, keepdims=False)

    gate_sum = share_of(gate_part, me)
    up_sum = share_of(up_part, me)
    for s in range(1, ways):
        owner = (me + s) % ways
        pair = jnp.stack([share_of(gate_part, owner), share_of(up_part, owner)]).astype(jnp.bfloat16)
        pair = lax.ppermute(pair, "dp", ring(ways, s))
        gate_sum = gate_sum + pair[0].astype(jnp.float32)
        up_sum = up_sum + pair[1].astype(jnp.float32)
    hidden_own = (jax.nn.silu(gate_sum) * up_sum).astype(jnp.bfloat16)
    hidden = jnp.zeros((expert_local, ways, share, hid), jnp.bfloat16)
    hidden = lax.dynamic_update_index_in_dim(hidden, hidden_own, me, 1)
    for s in range(1, ways):
        other = lax.ppermute(hidden_own, "dp", ring(ways, s))
        hidden = lax.dynamic_update_index_in_dim(hidden, other, (me - s) % ways, 1)
    hidden = hidden.reshape(expert_local, rows, hid)

    expert_out = jnp.einsum("erf,efd->erd", hidden, down_weight, preferred_element_type=jnp.float32)
    expert_out = expert_out.astype(jnp.bfloat16).reshape(1, expert_local, rows, width_local)
    returned = lax.all_to_all(expert_out, "expert", split_axis=2, concat_axis=0, tiled=True)
    returned = returned.reshape(experts_all * capacity, width_local)
    combine = (weight_expert[:, :, None] * placed.astype(jnp.float32)).reshape(
        tok_rows, experts_all * capacity
    )
    mixed = jnp.dot(
        combine,
        returned.astype(jnp.float32),
        precision=lax.Precision.HIGHEST,
        preferred_element_type=jnp.float32,
    )
    mixed = mixed.astype(jnp.bfloat16)

    synced = jnp.zeros((expert_local, ways, trained_rows, width_local), jnp.bfloat16)
    for expert, part in order:
        own = columns(own_source, expert, part, me)
        synced = lax.dynamic_update_slice(synced, own[None, None], (expert, me, part * piece, 0))
    for expert, part in order:
        for s in range(1, ways):
            arrival = arrivals[expert, part][s - 1]
            synced = lax.dynamic_update_slice(synced, arrival[None, None], (expert, (me - s) % ways, part * piece, 0))
    synced_down = synced.reshape(expert_local, ways * trained_rows, width_local)
    return (mixed, synced_down)


def solution(mesh):
    placed = (
        P("expert", "dp"),
        P("expert", None),
        P("expert", None),
        P("expert", "dp", None),
        P("expert", "dp", None),
        P("expert", None, "dp"),
        P("expert", "dp", None),
    )

    return jax.shard_map(
        local,
        mesh=mesh,
        in_specs=placed,
        out_specs=(P("expert", "dp"), P("expert", None, "dp")),
        check_vma=False,
    )
```

time: 170 us -> 121 us (0.71)
  waiting for transfers between devices: 93.3 us -> 31.8 us
  other arithmetic: 0.39 us -> 17.6 us
  between operations: 14.2 us -> 0.95 us
  local copies, waits for them, and re-layouts: 27.3 us -> 34.4 us
  starting transfers between devices: 18.2 us -> 24.4 us
  matrix products: 15.7 us -> 10.8 us
    psum x1 -> x0, waiting for transfers between devices: 85.6 us -> none  [local(): gate_sum, up_sum = lax.psum((gate_part, up_part), 'dp')]
    ppermute x0 -> x10, waiting for transfers between devices: none -> 23.4 us  [the longest x1 13.3 us: local(): pair = lax.ppermute(pair, 'dp', ring(ways, s))]
    squeeze x0 -> x2, local copies, waits for them, and re-layouts: none -> 14.3 us  [columns(): strip = source[expert, part * piece:(part + 1) * piece]]
    unnamed x7 -> x28, local copies, waits for them, and re-layouts: 13.4 us -> 0.93 us
    ppermute x0 -> x10, starting transfers between devices: none -> 11.2 us  [the longest x8 8.11 us: local(): lax.ppermute(columns(trained_down, expert, part, (me + s) % ways), 'dp',...]
    dynamic_update_slice x0 -> x9, local copies, waits for them, and re-layouts: none -> 11.2 us  [the longest x8 11.2 us: local(): lax.dynamic_update_slice(synced, arrival[None, None], (expert, (me - s) %...]
    all_to_all x1 -> x0, local copies, waits for them, and re-layouts: 10.5 us -> none  [local(): lax.all_to_all(narrowed, 'dp', split_axis=2, concat_axis=1, tiled=True)]
    convert_element_type x0 -> x9, other arithmetic: none -> 9.9 us  [the longest x8 9.74 us: columns(): return strip.astype(jnp.bfloat16)]
  transfers between devices with their start and end apart: 4 -> 12, of which waited for: 4 -> 3; matrix products, arithmetic and copies ran while one was open for 23% -> 49% of each run, Pallas kernels for 0% -> 0%
where the time goes in v1:
time: 121 us; the launch traced here: 120 us
  local copies, waits for them, and re-layouts  34.4 us (28%)
  waiting for transfers between devices  31.8 us (26%)
  starting transfers between devices  24.4 us (20%)
  other arithmetic  17.6 us (15%)
  matrix products  10.8 us (9%)
    squeeze x2, local copies, waits for them, and re-layouts, columns(): strip = source[expert, part * piece:(part + 1) * piece]  14.3 us
    ppermute x1, waiting for transfers between devices, local(): pair = lax.ppermute(pair, 'dp', ring(ways, s))  13.3 us
    dynamic_update_slice x8, local copies, waits for them, and re-layouts, local(): lax.dynamic_update_slice(synced, arrival[None, None], (expert, (me - s) %...  11.2 us
    ppermute x1, waiting for transfers between devices, local(): other = lax.ppermute(hidden_own, 'dp', ring(ways, s))  10.1 us
    convert_element_type x8, other arithmetic, columns(): return strip.astype(jnp.bfloat16)  9.74 us
    all_to_all x1, waiting for transfers between devices, local(): lax.all_to_all(expert_out, 'expert', split_axis=2, concat_axis=0, tiled=T...  8.39 us
    ppermute x8, starting transfers between devices, local(): lax.ppermute(columns(trained_down, expert, part, (me + s) % ways), 'dp',...  8.11 us
    all_to_all x1, starting transfers between devices, local(): lax.all_to_all(outgoing, 'expert', split_axis=0, concat_axis=2, tiled=True)  7.46 us
  transfers between devices with their start and end apart: 12, of which 3 were waited for; matrix products, arithmetic and copies ran while one was open for 49% of the time, Pallas kernels for 0%

profile of v1, /device:TPU:0, one launch (start us, length us, event | category | flops | bytes accessed | tf_op | source)
XLA Modules:
  0.0 120.0 jit_solution(7729707638794161970)
XLA Ops:
  0.6 0.8 copy.40
  1.4 0.1 convert_reduce_fusion
  1.6 0.1 copy.41
  1.7 0.1 copy.42
  1.8 0.1 eq.105
  2.0 0.3 convolution_convert_fusion.1
  2.4 1.0 reshape.121
  3.4 7.5 %all-to-all-start = ((bf16[16,4,4,1024]{3,2,1,0:T(4,128)(2,1)}), bf16[16,4,4,1024]{3,2,1,0:T(4,128)(2,1)}, u32[]{:S(2)}, u32[]{:S(2)}) async-start(bf16[16,4,4,1024]{3,2,1,0:T(4,128)(2,1)} %reshape.121), calls=%async_computation | async-start | bytes 1048576 | tf_op jit(solution)/shard_map/all_to_all | solution.py:55
  10.9 7.0 %slice_bitcast_fusion = (bf16[192,2048]{1,0:T(8,128)(2,1)}, bf16[192,2048]{1,0:T(8,128)(2,1)S(1)}, bf16[192,2048]{1,0:T(8,128)(2,1)S(1)}, bf16[192,2048]{1,0:T(8...) fusion(f32[4,384,2048]{2,1,0:T(8,128)} %param.13), kind=kLoop, calls=%fused_computation | loop fusion | bytes 12582912 | tf_op jit(solution)/shard_map/squeeze | solution.py:29
  17.9 1.9 %fusion.2 = bf16[192,1024]{1,0:T(8,128)(2,1)} fusion(bf16[192,2048]{1,0:T(8,128)(2,1)} %get-tuple-element.13, pred[]{:T(512)S(6)} %eq.109), kind=kLoop, calls=%fused_computation.23 | loop fusion | flops 196608 | bytes 1179649 | tf_op jit(solution)/shard_map/convert_element_type | solution.py:34
  19.8 1.5 %collective-permute-start.8 = (bf16[192,1024]{1,0:T(8,128)(2,1)}, bf16[192,1024]{1,0:T(8,128)(2,1)}, u32[]{:S(2)}, u32[]{:S(2)}) collective-permute-start(bf16[192,1024]{1,0:T(8,128)(2,1)} %fusion.2), channel_id=1, source_target_pairs={{0,16},{16,0},{1,17},{17,1},{2,18},{18,2},{3,19},{19,3},{4,20},{20... | collective-permute-start | bytes 1179656 | tf_op jit(solution)/shard_map/ppermute | solution.py:40
  21.3 1.9 %fusion.8 = bf16[192,1024]{1,0:T(8,128)(2,1)} fusion(bf16[192,2048]{1,0:T(8,128)(2,1)} %get-tuple-element.12, pred[]{:T(512)S(6)} %eq.109), kind=kLoop, calls=%fused_computation.35 | loop fusion | flops 196608 | bytes 1179649 | tf_op jit(solution)/shard_map/convert_element_type | solution.py:34
  23.2 0.5 collective-permute-start.2
  23.7 1.9 %fusion.7 = bf16[192,1024]{1,0:T(8,128)(2,1)} fusion(bf16[192,2048]{1,0:T(8,128)(2,1)} %get-tuple-element.11, pred[]{:T(512)S(6)} %eq.109), kind=kLoop, calls=%fused_computation.33 | loop fusion | flops 196608 | bytes 1179649 | tf_op jit(solution)/shard_map/convert_element_type | solution.py:34
  25.6 1.5 %collective-permute-start.3 = (bf16[192,1024]{1,0:T(8,128)(2,1)}, bf16[192,1024]{1,0:T(8,128)(2,1)}, u32[]{:S(2)}, u32[]{:S(2)}) collective-permute-start(bf16[192,1024]{1,0:T(8,128)(2,1)} %fusion.7), channel_id=1, source_target_pairs={{0,16},{16,0},{1,17},{17,1},{2,18},{18,2},{3,19},{19,3},{4,20},{20... | collective-permute-start | bytes 1179656 | tf_op jit(solution)/shard_map/ppermute | solution.py:40
  27.1 0.8 fusion.6
  27.9 0.5 collective-permute-start.4
  28.5 0.8 fusion.5
  29.3 1.5 %collective-permute-start.5 = (bf16[192,1024]{1,0:T(8,128)(2,1)}, bf16[192,1024]{1,0:T(8,128)(2,1)}, u32[]{:S(2)}, u32[]{:S(2)}) collective-permute-start(bf16[192,1024]{1,0:T(8,128)(2,1)} %fusion.5), channel_id=1, source_target_pairs={{0,16},{16,0},{1,17},{17,1},{2,18},{18,2},{3,19},{19,3},{4,20},{20... | collective-permute-start | bytes 1179656 | tf_op jit(solution)/shard_map/ppermute | solution.py:40
  30.8 0.1 copy.43
  30.8 7.3 %slice_bitcast_fusion.8 = (bf16[192,2048]{1,0:T(8,128)(2,1)S(1)}, bf16[192,2048]{1,0:T(8,128)(2,1)S(1)}, bf16[192,2048]{1,0:T(8,128)(2,1)}, bf16[192,2048]{1,0:T...) fusion(f32[4,384,2048]{2,1,0:T(8,128)} %param.13), kind=kLoop, calls=%fused_computation.8 | loop fusion | bytes 12582912 | tf_op jit(solution)/shard_map/squeeze | solution.py:29
  38.2 0.8 fusion.1
  39.0 0.8 fusion.3
  39.8 0.8 fusion.4
  40.6 3.5 %broadcast_in_dim.80 = bf16[4,2,384,1024]{3,2,1,0:T(8,128)(2,1)} broadcast(bf16[]{:T(256)} %constant.84.clone.1), dimensions={} | broadcast | bytes 6291458 | tf_op jit(solution)/shard_map/broadcast_in_dim | solution.py:97
  44.1 0.9 fusion.26
  45.0 0.9 fusion.28
  45.9 0.9 fusion.30
  46.8 0.9 fusion.32
  47.7 0.9 fusion.34
  48.6 0.9 fusion.36
  49.4 0.1 select_reduce_fusion
  49.6 0.1 copy.44
  49.7 0.9 fusion.38
  50.6 0.1 fusion.44
  50.7 0.9 fusion.40
  51.6 0.5 collective-permute-start.6
  52.1 1.8 %bitcast_dynamic-update-slice_fusion.7 = bf16[4,2,384,1024]{3,2,1,0:T(8,128)(2,1)} fusion(bf16[4,2,384,1024]{3,2,1,0:T(8,128)(2,1)} %fusion.40, s32[]{:T(128)S(6)} %select_n.152, bf16[192,1024]{1,0:T(8,128)(2,1)} %collective-permute-done.2), kind=kLoop, calls=%fused_computation.90 | loop fusion | bytes 786436 | tf_op jit(solution)/shard_map/dynamic_update_slice | solution.py:104
  53.9 1.2 %copy.45 = bf16[1,4,16,4,1024]{4,3,2,1,0:T(4,128)(2,1)S(1)} copy(bf16[1,4,16,4,1024]{4,3,1,2,0:T(4,128)(2,1)} %bitcast.4) | data formatting | bytes 1048576 | tf_op jit(solution)/shard_map/all_to_all | solution.py:55
  55.1 0.1 reshape.122
  55.3 4.1 %fusion.49 = f32[4,64,768]{2,1,0:T(8,128)S(1)} fusion(bf16[4,64,1024]{2,1,0:T(8,128)(2,1)S(1)} %reshape.122, bf16[4,1024,768]{2,1,0:T(8,128)(2,1)} %param.11), kind=kOutput, calls=%fused_computation.107 | convolution fusion | flops 402653184 | bytes 7602176 | tf_op jit(solution)/shard_map/erd,edf->erf/dot_general | solution.py:59
  59.4 4.1 %fusion.48 = f32[4,64,768]{2,1,0:T(8,128)S(1)} fusion(bf16[4,64,1024]{2,1,0:T(8,128)(2,1)S(1)} %reshape.122, bf16[4,1024,768]{2,1,0:T(8,128)(2,1)} %param.10), kind=kOutput, calls=%fused_computation.106 | convolution fusion | flops 402653184 | bytes 7602176 | tf_op jit(solution)/shard_map/erd,edf->erf/dot_general | solution.py:58
  63.6 1.6 %collective-permute-start = (bf16[2,4,32,768]{3,2,1,0:T(8,128)(2,1)S(1)}, bf16[2,4,32,768]{3,2,1,0:T(8,128)(2,1)S(1)}, u32[]{:S(2)}, u32[]{:S(2)}) collective-permute-start(bf16[2,4,32,768]{3,2,1,0:T(8,128)(2,1)S(1)} %pad_maximum_fusion), channel_id=1, source_target_pairs={{0,16},{16,0},{1,17},{17,1},{2,18},{18,2},{3,19},{19,3},{4,20},{20... | collective-permute-start | bytes 1179656 | tf_op jit(solution)/shard_map/ppermute | solution.py:71
  65.2 1.8 %bitcast_dynamic-update-slice_fusion.6 = bf16[4,2,384,1024]{3,2,1,0:T(8,128)(2,1)} fusion(bf16[4,2,384,1024]{3,2,1,0:T(8,128)(2,1)} %bitcast_dynamic-update-slice_fusion.7, s32[]{:T(128)S(6)} %select_n.152, bf16[192,1024]{1,0:T(8,128)(2,1)} %collective-permute-done.3), kind=kLoop, calls=%fused_computation.89 | loop fusion | bytes 786436 | tf_op jit(solution)/shard_map/dynamic_update_slice | solution.py:104
  66.9 0.5 collective-permute-start.7
  67.5 1.8 %bitcast_dynamic-update-slice_fusion.5 = bf16[4,2,384,1024]{3,2,1,0:T(8,128)(2,1)} fusion(bf16[4,2,384,1024]{3,2,1,0:T(8,128)(2,1)} %bitcast_dynamic-update-slice_fusion.6, s32[]{:T(128)S(6)} %select_n.152, bf16[192,1024]{1,0:T(8,128)(2,1)} %collective-permute-done.4), kind=kLoop, calls=%fused_computation.88 | loop fusion | bytes 786436 | tf_op jit(solution)/shard_map/dynamic_update_slice | solution.py:104
  69.2 13.3 %collective-permute-done = bf16[2,4,32,768]{3,2,1,0:T(8,128)(2,1)S(1)} collective-permute-done((bf16[2,4,32,768]{3,2,1,0:T(8,128)(2,1)S(1)}, bf16[2,4,32,768]{3,2,1,0:T(8,128)(2,1)S(1)}, u32[]{:S(2)}, u32[]{:S(2)}) %collective-permute-start) | collective-permute-done | bytes 393248 | tf_op jit(solution)/shard_map/ppermute | solution.py:71
  82.5 0.2 fusion.24
  82.7 1.6 %collective-permute-start.1 = (bf16[4,32,768]{2,1,0:T(8,128)(2,1)S(1)}, bf16[4,32,768]{2,1,0:T(8,128)(2,1)S(1)}, u32[]{:S(2)}, u32[]{:S(2)}) collective-permute-start(bf16[4,32,768]{2,1,0:T(8,128)(2,1)S(1)} %fusion.24), channel_id=1, source_target_pairs={{0,16},{16,0},{1,17},{17,1},{2,18},{18,2},{3,19},{19,3},{4,20},{20... | collective-permute-start | bytes 589832 | tf_op jit(solution)/shard_map/ppermute | solution.py:78
  84.3 0.2 bitcast_dynamic-update-slice_fusion.9
  84.4 10.1 %collective-permute-done.1 = bf16[4,32,768]{2,1,0:T(8,128)(2,1)S(1)} collective-permute-done((bf16[4,32,768]{2,1,0:T(8,128)(2,1)S(1)}, bf16[4,32,768]{2,1,0:T(8,128)(2,1)S(1)}, u32[]{:S(2)}, u32[]{:S(2)}) %collective-permute-start.1) | collective-permute-done | bytes 196640 | tf_op jit(solution)/shard_map/ppermute | solution.py:78
  94.5 1.5 %collective-permute-start.9 = (bf16[192,1024]{1,0:T(8,128)(2,1)S(1)}, bf16[192,1024]{1,0:T(8,128)(2,1)S(1)}, u32[]{:S(2)}, u32[]{:S(2)}) collective-permute-start(bf16[192,1024]{1,0:T(8,128)(2,1)S(1)} %copy-done.8), channel_id=1, source_target_pairs={{0,16},{16,0},{1,17},{17,1},{2,18},{18,2},{3,19},{19,3},{4,20},{20... | collective-permute-start | bytes 1179656 | tf_op jit(solution)/shard_map/ppermute | solution.py:40
  96.1 1.2 %fusion = bf16[1,4,64,1024]{3,2,1,0:T(8,128)(2,1)S(1)} fusion(bf16[4,64,768]{2,1,0:T(8,128)(2,1)S(1)} %bitcast.181, bf16[4,768,1024]{2,1,0:T(8,128)(2,1)S(1)} %bitcast.172), kind=kOutput, calls=%fused_computation.18 | convolution fusion | flops 402915328 | bytes 7208960 | tf_op jit(solution)/shard_map/erf,efd->erd/dot_general | solution.py:82
  97.3 1.2 %copy.51 = bf16[1,4,64,1024]{3,1,0,2:T(4,128)(2,1)} copy(bf16[1,4,64,1024]{3,2,1,0:T(8,128)(2,1)S(1)} %fusion) | data formatting | bytes 1048576 | tf_op jit(solution)/shard_map/reshape | solution.py:83
  98.5 5.7 %all-to-all-start.1 = ((bf16[1,4,64,1024]{3,1,0,2:T(4,128)(2,1)}), bf16[1,4,64,1024]{3,1,0,2:T(4,128)(2,1)S(1)}, u32[]{:S(2)}, u32[]{:S(2)}) async-start(bf16[1,4,64,1024]{3,1,0,2:T(4,128)(2,1)} %copy.51), calls=%async_computation.1 | async-start | bytes 1048576 | tf_op jit(solution)/shard_map/all_to_all | solution.py:84
  104.2 1.8 %bitcast_dynamic-update-slice_fusion.4 = bf16[4,2,384,1024]{3,2,1,0:T(8,128)(2,1)} fusion(bf16[4,2,384,1024]{3,2,1,0:T(8,128)(2,1)} %bitcast_dynamic-update-slice_fusion.5, s32[]{:T(128)S(6)} %select_n.152, bf16[192,1024]{1,0:T(8,128)(2,1)} %collective-permute-done.5), kind=kLoop, calls=%fused_computation.87 | loop fusion | bytes 786436 | tf_op jit(solution)/shard_map/dynamic_update_slice | solution.py:104
  106.0 0.8 bitcast_dynamic-update-slice_fusion.3
  106.8 0.8 bitcast_dynamic-update-slice_fusion.2
  107.6 1.8 %bitcast_dynamic-update-slice_fusion.1 = bf16[4,2,384,1024]{3,2,1,0:T(8,128)(2,1)} fusion(bf16[4,2,384,1024]{3,2,1,0:T(8,128)(2,1)} %bitcast_dynamic-update-slice_fusion.2, s32[]{:T(128)S(6)} %select_n.152, bf16[192,1024]{1,0:T(8,128)(2,1)} %collective-permute-done.8), kind=kLoop, calls=%fused_computation.84 | loop fusion | bytes 786436 | tf_op jit(solution)/shard_map/dynamic_update_slice | solution.py:104
  109.3 0.8 bitcast_dynamic-update-slice_fusion
  110.1 8.4 %all-to-all-done.1 = bf16[1,4,64,1024]{3,1,0,2:T(4,128)(2,1)S(1)} async-done(((bf16[1,4,64,1024]{3,1,0,2:T(4,128)(2,1)}), bf16[1,4,64,1024]{3,1,0,2:T(4,128)(2,1)S(1)}, u32[]{:S(2)}, u32[]{:S(2)}) %all-to-all-start.1) | async-done | bytes 524320 | tf_op jit(solution)/shard_map/all_to_all | solution.py:84
  118.5 0.3 copy.57
  118.8 0.1 reshape.127
  118.9 1.0 convolution_convert_fusion.2
  (46 shorter events, 0.4 us)
Async XLA Ops:
  0.6 1.4 %copy-start = (bf16[32,1024]{1,0:T(8,128)(2,1)S(1)}, bf16[32,1024]{1,0:T(8,128)(2,1)}, u32[]{:S(2)}) copy-start(bf16[32,1024]{1,0:T(8,128)(2,1)} %param.7) | copy-start | bytes 196612
  3.4 50.5 %all-to-all-start = ((bf16[16,4,4,1024]{3,2,1,0:T(4,128)(2,1)}), bf16[16,4,4,1024]{3,2,1,0:T(4,128)(2,1)}, u32[]{:S(2)}, u32[]{:S(2)}) async-start(bf16[16,4,4,1024]{3,2,1,0:T(4,128)(2,1)} %reshape.121), calls=%async_computation | async-start | bytes 1048576 | tf_op jit(solution)/shard_map/all_to_all | solution.py:55
  10.8 19.9 %copy-start.10 = (f32[32,8]{0,1:T(8,128)S(1)}, f32[32,8]{0,1:T(8,128)}, u32[]{:S(2)}) copy-start(f32[32,8]{0,1:T(8,128)} %param.9) | copy-start | bytes 3076
  19.8 87.8 %collective-permute-start.8 = (bf16[192,1024]{1,0:T(8,128)(2,1)}, bf16[192,1024]{1,0:T(8,128)(2,1)}, u32[]{:S(2)}, u32[]{:S(2)}) collective-permute-start(bf16[192,1024]{1,0:T(8,128)(2,1)} %fusion.2), channel_id=1, source_target_pairs={{0,16},{16,0},{1,17},{17,1},{2,18},{18,2},{3,19},{19,3},{4,20},{20... | collective-permute-start | bytes 1179656 | tf_op jit(solution)/shard_map/ppermute | solution.py:40
  23.2 28.4 %collective-permute-start.2 = (bf16[192,1024]{1,0:T(8,128)(2,1)}, bf16[192,1024]{1,0:T(8,128)(2,1)}, u32[]{:S(2)}, u32[]{:S(2)}) collective-permute-start(bf16[192,1024]{1,0:T(8,128)(2,1)} %fusion.8), channel_id=1, source_target_pairs={{0,16},{16,0},{1,17},{17,1},{2,18},{18,2},{3,19},{19,3},{4,20},{20... | collective-permute-start | bytes 1179656 | tf_op jit(solution)/shard_map/ppermute | solution.py:40
  25.6 38.0 %collective-permute-start.3 = (bf16[192,1024]{1,0:T(8,128)(2,1)}, bf16[192,1024]{1,0:T(8,128)(2,1)}, u32[]{:S(2)}, u32[]{:S(2)}) collective-permute-start(bf16[192,1024]{1,0:T(8,128)(2,1)} %fusion.7), channel_id=1, source_target_pairs={{0,16},{16,0},{1,17},{17,1},{2,18},{18,2},{3,19},{19,3},{4,20},{20... | collective-permute-start | bytes 1179656 | tf_op jit(solution)/shard_map/ppermute | solution.py:40
  27.9 39.0 %collective-permute-start.4 = (bf16[192,1024]{1,0:T(8,128)(2,1)}, bf16[192,1024]{1,0:T(8,128)(2,1)}, u32[]{:S(2)}, u32[]{:S(2)}) collective-permute-start(bf16[192,1024]{1,0:T(8,128)(2,1)} %fusion.6), channel_id=1, source_target_pairs={{0,16},{16,0},{1,17},{17,1},{2,18},{18,2},{3,19},{19,3},{4,20},{20... | collective-permute-start | bytes 1179656 | tf_op jit(solution)/shard_map/ppermute | solution.py:40
  29.3 75.0 %collective-permute-start.5 = (bf16[192,1024]{1,0:T(8,128)(2,1)}, bf16[192,1024]{1,0:T(8,128)(2,1)}, u32[]{:S(2)}, u32[]{:S(2)}) collective-permute-start(bf16[192,1024]{1,0:T(8,128)(2,1)} %fusion.5), channel_id=1, source_target_pairs={{0,16},{16,0},{1,17},{17,1},{2,18},{18,2},{3,19},{19,3},{4,20},{20... | collective-permute-start | bytes 1179656 | tf_op jit(solution)/shard_map/ppermute | solution.py:40
  30.8 7.3 %copy-start.1 = (bf16[192,2048]{1,0:T(8,128)(2,1)S(1)}, bf16[192,2048]{1,0:T(8,128)(2,1)}, u32[]{:S(2)}) copy-start(bf16[192,2048]{1,0:T(8,128)(2,1)} %get-tuple-element.6) | copy-start | bytes 2359300
  39.8 7.9 %copy-start.3 = (bf16[192,2048]{1,0:T(8,128)(2,1)S(1)}, bf16[192,2048]{1,0:T(8,128)(2,1)}, u32[]{:S(2)}) copy-start(bf16[192,2048]{1,0:T(8,128)(2,1)} %get-tuple-element.17) | copy-start | bytes 2359300
  40.6 8.0 %copy-start.2 = (bf16[192,2048]{1,0:T(8,128)(2,1)S(1)}, bf16[192,2048]{1,0:T(8,128)(2,1)}, u32[]{:S(2)}) copy-start(bf16[192,2048]{1,0:T(8,128)(2,1)} %get-tuple-element.16) | copy-start | bytes 2359300
  40.6 3.5 %copy-start.7 = (bf16[192,2048]{1,0:T(8,128)(2,1)S(1)}, bf16[192,2048]{1,0:T(8,128)(2,1)}, u32[]{:S(2)}) copy-start(bf16[192,2048]{1,0:T(8,128)(2,1)} %get-tuple-element.21) | copy-start | bytes 2359300
  40.6 4.4 %copy-start.6 = (bf16[192,2048]{1,0:T(8,128)(2,1)S(1)}, bf16[192,2048]{1,0:T(8,128)(2,1)}, u32[]{:S(2)}) copy-start(bf16[192,2048]{1,0:T(8,128)(2,1)} %get-tuple-element.20) | copy-start | bytes 2359300
  40.6 5.3 %copy-start.5 = (bf16[192,2048]{1,0:T(8,128)(2,1)S(1)}, bf16[192,2048]{1,0:T(8,128)(2,1)}, u32[]{:S(2)}) copy-start(bf16[192,2048]{1,0:T(8,128)(2,1)} %get-tuple-element.19) | copy-start | bytes 2359300
  40.6 6.2 %copy-start.4 = (bf16[192,2048]{1,0:T(8,128)(2,1)S(1)}, bf16[192,2048]{1,0:T(8,128)(2,1)}, u32[]{:S(2)}) copy-start(bf16[192,2048]{1,0:T(8,128)(2,1)} %get-tuple-element.18) | copy-start | bytes 2359300
  51.6 54.5 %collective-permute-start.6 = (bf16[192,1024]{1,0:T(8,128)(2,1)}, bf16[192,1024]{1,0:T(8,128)(2,1)S(1)}, u32[]{:S(2)}, u32[]{:S(2)}) collective-permute-start(bf16[192,1024]{1,0:T(8,128)(2,1)} %fusion.4), channel_id=1, source_target_pairs={{0,16},{16,0},{1,17},{17,1},{2,18},{18,2},{3,19},{19,3},{4,20},{20... | collective-permute-start | bytes 1179656 | tf_op jit(solution)/shard_map/ppermute | solution.py:40
  55.2 40.8 %slice-start = ((s8[6291456]{0:T(1024)(128)(4,1)}), s8[4194304]{0:T(1024)(128)(4,1)S(1)}, s32[]{:S(2)}) async-start(s8[6291456]{0:T(1024)(128)(4,1)} %bitcast.171), calls=%async_computation.2 | async-start | bytes 8388608
  59.4 7.6 %copy-start.9 = (bf16[192,1024]{1,0:T(8,128)(2,1)S(1)}, bf16[192,1024]{1,0:T(8,128)(2,1)}, u32[]{:S(2)}) copy-start(bf16[192,1024]{1,0:T(8,128)(2,1)} %fusion.3) | copy-start | bytes 1179652
  59.4 35.2 %copy-start.8 = (bf16[192,1024]{1,0:T(8,128)(2,1)S(1)}, bf16[192,1024]{1,0:T(8,128)(2,1)}, u32[]{:S(2)}) copy-start(bf16[192,1024]{1,0:T(8,128)(2,1)} %fusion.1) | copy-start | bytes 1179652
  59.4 36.7 %slice-start.1 = ((s8[6291456]{0:T(1024)(128)(4,1)}), s8[2097152]{0:T(1024)(128)(4,1)S(1)}, s32[]{:S(2)}) async-start(s8[6291456]{0:T(1024)(128)(4,1)} %bitcast.171), calls=%async_computation.3 | async-start | bytes 4194304
  63.6 18.9 %collective-permute-start = (bf16[2,4,32,768]{3,2,1,0:T(8,128)(2,1)S(1)}, bf16[2,4,32,768]{3,2,1,0:T(8,128)(2,1)S(1)}, u32[]{:S(2)}, u32[]{:S(2)}) collective-permute-start(bf16[2,4,32,768]{3,2,1,0:T(8,128)(2,1)S(1)} %pad_maximum_fusion), channel_id=1, source_target_pairs={{0,16},{16,0},{1,17},{17,1},{2,18},{18,2},{3,19},{19,3},{4,20},{20... | collective-permute-start | bytes 1179656 | tf_op jit(solution)/shard_map/ppermute | solution.py:71
  66.9 39.9 %collective-permute-start.7 = (bf16[192,1024]{1,0:T(8,128)(2,1)S(1)}, bf16[192,1024]{1,0:T(8,128)(2,1)S(1)}, u32[]{:S(2)}, u32[]{:S(2)}) collective-permute-start(bf16[192,1024]{1,0:T(8,128)(2,1)S(1)} %copy-done.9), channel_id=1, source_target_pairs={{0,16},{16,0},{1,17},{17,1},{2,18},{18,2},{3,19},{19,3},{4,20},{20... | collective-permute-start | bytes 1179656 | tf_op jit(solution)/shard_map/ppermute | solution.py:40
  82.7 11.9 %collective-permute-start.1 = (bf16[4,32,768]{2,1,0:T(8,128)(2,1)S(1)}, bf16[4,32,768]{2,1,0:T(8,128)(2,1)S(1)}, u32[]{:S(2)}, u32[]{:S(2)}) collective-permute-start(bf16[4,32,768]{2,1,0:T(8,128)(2,1)S(1)} %fusion.24), channel_id=1, source_target_pairs={{0,16},{16,0},{1,17},{17,1},{2,18},{18,2},{3,19},{19,3},{4,20},{20... | collective-permute-start | bytes 589832 | tf_op jit(solution)/shard_map/ppermute | solution.py:78
  94.5 14.8 %collective-permute-start.9 = (bf16[192,1024]{1,0:T(8,128)(2,1)S(1)}, bf16[192,1024]{1,0:T(8,128)(2,1)S(1)}, u32[]{:S(2)}, u32[]{:S(2)}) collective-permute-start(bf16[192,1024]{1,0:T(8,128)(2,1)S(1)} %copy-done.8), channel_id=1, source_target_pairs={{0,16},{16,0},{1,17},{17,1},{2,18},{18,2},{3,19},{19,3},{4,20},{20... | collective-permute-start | bytes 1179656 | tf_op jit(solution)/shard_map/ppermute | solution.py:40
  98.5 20.0 %all-to-all-start.1 = ((bf16[1,4,64,1024]{3,1,0,2:T(4,128)(2,1)}), bf16[1,4,64,1024]{3,1,0,2:T(4,128)(2,1)S(1)}, u32[]{:S(2)}, u32[]{:S(2)}) async-start(bf16[1,4,64,1024]{3,1,0,2:T(4,128)(2,1)} %copy.51), calls=%async_computation.1 | async-start | bytes 1048576 | tf_op jit(solution)/shard_map/all_to_all | solution.py:84

commit v2 on v1

--- a/solution.py
+++ b/solution.py
@@ -1,6 +1,8 @@
 import jax
 import jax.numpy as jnp
 from jax import lax
+from jax.experimental import pallas as pl
+from jax.experimental.pallas import tpu as pltpu
 from jax.sharding import PartitionSpec as P
 
 
@@ -10,6 +12,45 @@
 
 def ring(size, shift):
     return [(i, (i + shift) % size) for i in range(size)]
+
+
+def narrow(where, trained, synced, expert, part, piece, ways, width):
+    experts, trained_rows, _ = trained.shape
+    step = 64 if piece % 64 == 0 else piece
+    steps = piece // step
+
+    def body(where_ref, strip_ref, *refs):
+        sent_ref, own_ref = refs[-2:]
+        for s in range(ways):
+            owner = lax.rem(where_ref[0] + s, ways)
+            columns = strip_ref[0, :, pl.ds(pl.multiple_of(owner * width, 128), width)]
+            if s:
+                sent_ref[s - 1] = columns.astype(jnp.bfloat16)
+            else:
+                own_ref[0, 0] = columns.astype(jnp.bfloat16)
+
+    in_specs = [pl.BlockSpec((1, step, ways * width), lambda i, w: (expert, part * steps + i, 0))]
+    operands = [where, trained]
+    if synced is not None:
+        in_specs.append(pl.BlockSpec(memory_space=pl.ANY))
+        operands.append(synced)
+    return pl.pallas_call(
+        body,
+        grid_spec=pltpu.PrefetchScalarGridSpec(
+            num_scalar_prefetch=1,
+            grid=(steps,),
+            in_specs=in_specs,
+            out_specs=[
+                pl.BlockSpec((ways - 1, step, width), lambda i, w: (0, i, 0)),
+                pl.BlockSpec((1, 1, step, width), lambda i, w: (expert, w[0], part * steps + i, 0)),
+            ],
+        ),
+        out_shape=[
+            jax.ShapeDtypeStruct((ways - 1, piece, width), jnp.bfloat16),
+            jax.ShapeDtypeStruct((experts, ways, trained_rows, width), jnp.bfloat16),
+        ],
+        input_output_aliases={} if synced is None else {2: 1},
+    )(*operands)
 
 
 def local(tokens, routes, route_weight, gate_weight, up_weight, down_weight, trained_down):
@@ -23,22 +64,17 @@
     capacity = CAP
     rows = groups * capacity
     share = rows // ways
-    piece = trained_rows // PIECES
-
-    def columns(source, expert, part, owner):
-        strip = source[expert, part * piece:(part + 1) * piece]
-        if ways == 2:
-            strip = jnp.where(owner == 0, strip[:, :width_local], strip[:, width_local:])
-        else:
-            strip = lax.dynamic_slice_in_dim(strip, owner * width_local, width_local, 1)
-        return strip.astype(jnp.bfloat16)
+    pieces = PIECES if trained_rows % (16 * PIECES) == 0 else 1
+    piece = trained_rows // pieces
+    where = me.astype(jnp.int32).reshape(1)
 
     arrivals = {}
-    order = [(e, p) for e in range(expert_local) for p in range(PIECES)]
+    synced = None
+    order = [(e, p) for e in range(expert_local) for p in range(pieces)]
     for expert, part in order:
+        sent, synced = narrow(where, trained_down, synced, expert, part, piece, ways, width_local)
         arrivals[expert, part] = [
-            lax.ppermute(columns(trained_down, expert, part, (me + s) % ways), "dp", ring(ways, s))
-            for s in range(1, ways)
+            lax.ppermute(sent[s - 1], "dp", ring(ways, s)) for s in range(1, ways)
         ]
 
     labels = lax.broadcasted_iota(jnp.int32, (1, 1, experts_all), 2)
@@ -50,7 +86,6 @@
     placed = (counts[:, :, None] == 1) & (earlier[:, :, None] == slot_ids)
     dispatch = placed.astype(jnp.bfloat16).reshape(tok_rows, experts_all * capacity)
     outgoing = jnp.dot(dispatch.T, tokens, preferred_element_type=jnp.float32).astype(jnp.bfloat16)
-    own_source, outgoing = lax.optimization_barrier((trained_down, outgoing))
     outgoing = outgoing.reshape(groups, expert_local, capacity, width_local)
     arrived = lax.all_to_all(outgoing, "expert", split_axis=0, concat_axis=2, tiled=True)
     arrived = arrived.reshape(expert_local, rows, width_local)
@@ -94,10 +129,6 @@
     )
     mixed = mixed.astype(jnp.bfloat16)
 
-    synced = jnp.zeros((expert_local, ways, trained_rows, width_local), jnp.bfloat16)
-    for expert, part in order:
-        own = columns(own_source, expert, part, me)
-        synced = lax.dynamic_update_slice(synced, own[None, None], (expert, me, part * piece, 0))
     for expert, part in order:
         for s in range(1, ways):
             arrival = arrivals[expert, part][s - 1]

time: 121 us -> 115 us (0.950)
  Pallas kernels: 0 us -> 24.5 us
  local copies, waits for them, and re-layouts: 34.4 us -> 10.5 us
  other arithmetic: 17.6 us -> 0.75 us
  waiting for transfers between devices: 31.8 us -> 42.3 us
    pallas_call x0 -> x8, Pallas kernels: none -> 24.5 us  [narrow(): pl.pallas_call(body, grid_spec=pltpu.PrefetchScalarGridSpec(num_scalar_pr...]
    squeeze x2 -> x0, local copies, waits for them, and re-layouts: 14.3 us -> none  [columns(): strip = source[expert, part * piece:(part + 1) * piece]]
    convert_element_type x8 -> x0, other arithmetic: 9.74 us -> none  [columns(): return strip.astype(jnp.bfloat16)]
    ppermute x1, waiting for transfers between devices: 13.3 us -> 21.7 us  [local(): pair = lax.ppermute(pair, 'dp', ring(ways, s))]
    dynamic_update_slice x8 -> x0, other arithmetic: 7.13 us -> none  [local(): lax.dynamic_update_slice(synced, own[None, None], (expert, me, part * pie...]
    dynamic_update_slice x8, local copies, waits for them, and re-layouts: 11.2 us -> 6.18 us  [local(): lax.dynamic_update_slice(synced, arrival[None, None], (expert, (me - s) %...]
    broadcast_in_dim x1 -> x0, local copies, waits for them, and re-layouts: 3.51 us -> none  [local(): jnp.zeros((expert_local, ways, trained_rows, width_local), jnp.bfloat16)]
    all_to_all x1, waiting for transfers between devices: 8.39 us -> 10.4 us  [local(): lax.all_to_all(expert_out, 'expert', split_axis=2, concat_axis=0, tiled=T...]
  transfers between devices with their start and end apart: 12 -> 12, of which waited for: 3 -> 3; matrix products, arithmetic and copies ran while one was open for 49% -> 16% of each run, Pallas kernels for 0% -> 21%
where the time goes in v2:
time: 115 us; the launch traced here: 114 us
  waiting for transfers between devices  42.3 us (37%)
  Pallas kernels  24.5 us (21%)
  starting transfers between devices  24.4 us (21%)
  matrix products  10.8 us (9%)
  local copies, waits for them, and re-layouts  10.5 us (9%)
    pallas_call x8, Pallas kernels, narrow(): pl.pallas_call(body, grid_spec=pltpu.PrefetchScalarGridSpec(num_scalar_pr...  24.5 us
    ppermute x1, waiting for transfers between devices, local(): pair = lax.ppermute(pair, 'dp', ring(ways, s))  21.7 us
    all_to_all x1, waiting for transfers between devices, local(): lax.all_to_all(expert_out, 'expert', split_axis=2, concat_axis=0, tiled=T...  10.4 us
    ppermute x1, waiting for transfers between devices, local(): other = lax.ppermute(hidden_own, 'dp', ring(ways, s))  10.2 us
    ppermute x8, starting transfers between devices, local(): lax.ppermute(sent[s - 1], 'dp', ring(ways, s))  8.17 us
    all_to_all x1, starting transfers between devices, local(): lax.all_to_all(outgoing, 'expert', split_axis=0, concat_axis=2, tiled=True)  7.41 us
    dynamic_update_slice x8, local copies, waits for them, and re-layouts, local(): lax.dynamic_update_slice(synced, arrival[None, None], (expert, (me - s) %...  6.18 us
    all_to_all x1, starting transfers between devices, local(): lax.all_to_all(expert_out, 'expert', split_axis=2, concat_axis=0, tiled=T...  5.71 us
  transfers between devices with their start and end apart: 12, of which 3 were waited for; matrix products, arithmetic and copies ran while one was open for 16% of the time, Pallas kernels for 21%

profile of v2, /device:TPU:0, one launch (start us, length us, event | category | flops | bytes accessed | tf_op | source)
XLA Modules:
  0.0 114.1 jit_solution(8026400543577503322)
XLA Ops:
  0.6 0.0 copy-start
  0.6 0.8 copy.47
  1.4 0.1 convert_reduce_fusion
  1.6 0.1 reduce_window_sum.11
  1.6 0.1 copy.49
  1.7 0.1 copy.48
  1.8 0.1 eq.77
  2.0 0.3 convolution_convert_fusion.1
  2.4 1.0 reshape.124
  3.4 7.4 %all-to-all-start = ((bf16[16,4,4,1024]{3,2,1,0:T(4,128)(2,1)}), bf16[16,4,4,1024]{3,2,1,0:T(4,128)(2,1)S(1)}, u32[]{:S(2)}, u32[]{:S(2)}) async-start(bf16[16,4,4,1024]{3,2,1,0:T(4,128)(2,1)} %reshape.124), calls=%async_computation | async-start | bytes 1048576 | tf_op jit(solution)/shard_map/all_to_all | solution.py:90
  10.8 3.1 %shard_map.86 = (bf16[1,192,1024]{2,1,0:T(8,128)(2,1)}, bf16[4,2,384,1024]{3,2,1,0:T(8,128)(2,1)}) custom-call(s32[1]{0:T(128)} %bitcast.22.where_ref, f32[4,384,2048]{2,1,0:T(8,128)} %strip_ref.15), custom_call_target="tpu_custom_call" | custom-call | tf_op jit(solution)/shard_map/pallas_call | solution.py:37
  13.9 1.5 %collective-permute-start.2 = (bf16[192,1024]{1,0:T(8,128)(2,1)}, bf16[192,1024]{1,0:T(8,128)(2,1)S(1)}, u32[]{:S(2)}, u32[]{:S(2)}) collective-permute-start(bf16[192,1024]{1,0:T(8,128)(2,1)} %bitcast.137), channel_id=1, source_target_pairs={{0,16},{16,0},{1,17},{17,1},{2,18},{18,2},{3,19},{19,3},{4,20},{20... | collective-permute-start | bytes 1179656 | tf_op jit(solution)/shard_map/ppermute | solution.py:77
  15.4 3.1 %shard_map.87 = (bf16[1,192,1024]{2,1,0:T(8,128)(2,1)}, bf16[4,2,384,1024]{3,2,1,0:T(8,128)(2,1)}) custom-call(s32[1]{0:T(128)} %bitcast.22.where_ref, f32[4,384,2048]{2,1,0:T(8,128)} %strip_ref.15, bf16[4,2,384,1024]{3,2,1,0:T(8,128)(2,1)} %get-tuple-element.18.refs_0_), custom_call_target="tpu_custom_call", output_to_operand_aliasing={{1}: (2, {})} | custom-call | tf_op jit(solution)/shard_map/pallas_call | solution.py:37
  18.4 0.5 collective-permute-start.3
  19.0 3.1 %shard_map.88 = (bf16[1,192,1024]{2,1,0:T(8,128)(2,1)}, bf16[4,2,384,1024]{3,2,1,0:T(8,128)(2,1)}) custom-call(s32[1]{0:T(128)} %bitcast.22.where_ref, f32[4,384,2048]{2,1,0:T(8,128)} %strip_ref.15, bf16[4,2,384,1024]{3,2,1,0:T(8,128)(2,1)} %get-tuple-element.19.refs_0_), custom_call_target="tpu_custom_call", output_to_operand_aliasing={{1}: (2, {})} | custom-call | tf_op jit(solution)/shard_map/pallas_call | solution.py:37
  22.0 1.5 %collective-permute-start.4 = (bf16[192,1024]{1,0:T(8,128)(2,1)}, bf16[192,1024]{1,0:T(8,128)(2,1)S(1)}, u32[]{:S(2)}, u32[]{:S(2)}) collective-permute-start(bf16[192,1024]{1,0:T(8,128)(2,1)} %bitcast.133), channel_id=1, source_target_pairs={{0,16},{16,0},{1,17},{17,1},{2,18},{18,2},{3,19},{19,3},{4,20},{20... | collective-permute-start | bytes 1179656 | tf_op jit(solution)/shard_map/ppermute | solution.py:77
  23.5 3.1 %shard_map.89 = (bf16[1,192,1024]{2,1,0:T(8,128)(2,1)}, bf16[4,2,384,1024]{3,2,1,0:T(8,128)(2,1)}) custom-call(s32[1]{0:T(128)} %bitcast.22.where_ref, f32[4,384,2048]{2,1,0:T(8,128)} %strip_ref.15, bf16[4,2,384,1024]{3,2,1,0:T(8,128)(2,1)} %get-tuple-element.20.refs_0_), custom_call_target="tpu_custom_call", output_to_operand_aliasing={{1}: (2, {})} | custom-call | tf_op jit(solution)/shard_map/pallas_call | solution.py:37
  26.6 0.5 collective-permute-start.5
  27.1 3.1 %shard_map.90 = (bf16[1,192,1024]{2,1,0:T(8,128)(2,1)}, bf16[4,2,384,1024]{3,2,1,0:T(8,128)(2,1)}) custom-call(s32[1]{0:T(128)} %bitcast.22.where_ref, f32[4,384,2048]{2,1,0:T(8,128)} %strip_ref.15, bf16[4,2,384,1024]{3,2,1,0:T(8,128)(2,1)} %get-tuple-element.21.refs_0_), custom_call_target="tpu_custom_call", output_to_operand_aliasing={{1}: (2, {})} | custom-call | tf_op jit(solution)/shard_map/pallas_call | solution.py:37
  30.2 1.5 %collective-permute-start.6 = (bf16[192,1024]{1,0:T(8,128)(2,1)}, bf16[192,1024]{1,0:T(8,128)(2,1)S(1)}, u32[]{:S(2)}, u32[]{:S(2)}) collective-permute-start(bf16[192,1024]{1,0:T(8,128)(2,1)} %bitcast.132), channel_id=1, source_target_pairs={{0,16},{16,0},{1,17},{17,1},{2,18},{18,2},{3,19},{19,3},{4,20},{20... | collective-permute-start | bytes 1179656 | tf_op jit(solution)/shard_map/ppermute | solution.py:77
  31.6 3.1 %shard_map.91 = (bf16[1,192,1024]{2,1,0:T(8,128)(2,1)}, bf16[4,2,384,1024]{3,2,1,0:T(8,128)(2,1)}) custom-call(s32[1]{0:T(128)} %bitcast.22.where_ref, f32[4,384,2048]{2,1,0:T(8,128)} %strip_ref.15, bf16[4,2,384,1024]{3,2,1,0:T(8,128)(2,1)} %get-tuple-element.22.refs_0_), custom_call_target="tpu_custom_call", output_to_operand_aliasing={{1}: (2, {})} | custom-call | tf_op jit(solution)/shard_map/pallas_call | solution.py:37
  34.7 3.1 %shard_map.92 = (bf16[1,192,1024]{2,1,0:T(8,128)(2,1)}, bf16[4,2,384,1024]{3,2,1,0:T(8,128)(2,1)}) custom-call(s32[1]{0:T(128)} %bitcast.22.where_ref, f32[4,384,2048]{2,1,0:T(8,128)} %strip_ref.15, bf16[4,2,384,1024]{3,2,1,0:T(8,128)(2,1)} %get-tuple-element.23.refs_0_), custom_call_target="tpu_custom_call", output_to_operand_aliasing={{1}: (2, {})} | custom-call | tf_op jit(solution)/shard_map/pallas_call | solution.py:37
  37.8 3.1 %shard_map.93 = (bf16[1,192,1024]{2,1,0:T(8,128)(2,1)}, bf16[4,2,384,1024]{3,2,1,0:T(8,128)(2,1)}) custom-call(s32[1]{0:T(128)} %bitcast.22.where_ref, f32[4,384,2048]{2,1,0:T(8,128)} %strip_ref.15, bf16[4,2,384,1024]{3,2,1,0:T(8,128)(2,1)} %get-tuple-element.24.refs_0_), custom_call_target="tpu_custom_call", output_to_operand_aliasing={{1}: (2, {})} | custom-call | tf_op jit(solution)/shard_map/pallas_call | solution.py:37
  40.9 0.1 copy.50
  40.9 0.1 select_reduce_fusion
  41.1 0.1 copy.51
  41.2 0.1 fusion.12
  41.2 0.0 collective-permute-done.2
  41.2 0.6 collective-permute-start.7
  41.8 0.8 bitcast_dynamic-update-slice_fusion.7
  42.6 0.0 all-to-all-done
  42.6 0.2 copy.52
  42.8 0.1 reshape.125
  43.0 0.0 slice-start
  43.0 4.1 %fusion.16 = f32[4,64,768]{2,1,0:T(8,128)S(1)} fusion(bf16[4,64,1024]{2,1,0:T(8,128)(2,1)S(1)} %reshape.125, bf16[4,1024,768]{2,1,0:T(8,128)(2,1)} %param.10), kind=kOutput, calls=%fused_computation.42 | convolution fusion | flops 402653184 | bytes 7602176 | tf_op jit(solution)/shard_map/erd,edf->erf/dot_general | solution.py:93
  47.1 0.0 slice-start.1
  47.1 4.1 %fusion.17 = f32[4,64,768]{2,1,0:T(8,128)S(1)} fusion(bf16[4,64,1024]{2,1,0:T(8,128)(2,1)S(1)} %reshape.125, bf16[4,1024,768]{2,1,0:T(8,128)(2,1)} %param.11), kind=kOutput, calls=%fused_computation.43 | convolution fusion | flops 402653184 | bytes 7602176 | tf_op jit(solution)/shard_map/erd,edf->erf/dot_general | solution.py:94
  51.2 0.1 fusion.9
  51.3 0.0 collective-permute-done.3
  51.3 1.6 %collective-permute-start = (bf16[2,4,32,768]{3,2,1,0:T(8,128)(2,1)S(1)}, bf16[2,4,32,768]{3,2,1,0:T(8,128)(2,1)S(1)}, u32[]{:S(2)}, u32[]{:S(2)}) collective-permute-start(bf16[2,4,32,768]{3,2,1,0:T(8,128)(2,1)S(1)} %pad_maximum_fusion), channel_id=1, source_target_pairs={{0,16},{16,0},{1,17},{17,1},{2,18},{18,2},{3,19},{19,3},{4,20},{20... | collective-permute-start | bytes 1179656 | tf_op jit(solution)/shard_map/ppermute | solution.py:106
  52.9 0.8 bitcast_dynamic-update-slice_fusion.6
  53.6 0.0 collective-permute-done.4
  53.6 0.5 collective-permute-start.8
  54.2 0.8 bitcast_dynamic-update-slice_fusion.5
  54.9 21.7 %collective-permute-done = bf16[2,4,32,768]{3,2,1,0:T(8,128)(2,1)S(1)} collective-permute-done((bf16[2,4,32,768]{3,2,1,0:T(8,128)(2,1)S(1)}, bf16[2,4,32,768]{3,2,1,0:T(8,128)(2,1)S(1)}, u32[]{:S(2)}, u32[]{:S(2)}) %collective-permute-start) | collective-permute-done | bytes 393248 | tf_op jit(solution)/shard_map/ppermute | solution.py:106
  76.6 0.2 fusion.8
  76.8 1.6 %collective-permute-start.1 = (bf16[4,32,768]{2,1,0:T(8,128)(2,1)S(1)}, bf16[4,32,768]{2,1,0:T(8,128)(2,1)S(1)}, u32[]{:S(2)}, u32[]{:S(2)}) collective-permute-start(bf16[4,32,768]{2,1,0:T(8,128)(2,1)S(1)} %fusion.8), channel_id=1, source_target_pairs={{0,16},{16,0},{1,17},{17,1},{2,18},{18,2},{3,19},{19,3},{4,20},{20... | collective-permute-start | bytes 589832 | tf_op jit(solution)/shard_map/ppermute | solution.py:113
  78.4 0.2 bitcast_dynamic-update-slice_fusion.9
  78.5 10.2 %collective-permute-done.1 = bf16[4,32,768]{2,1,0:T(8,128)(2,1)S(1)} collective-permute-done((bf16[4,32,768]{2,1,0:T(8,128)(2,1)S(1)}, bf16[4,32,768]{2,1,0:T(8,128)(2,1)S(1)}, u32[]{:S(2)}, u32[]{:S(2)}) %collective-permute-start.1) | collective-permute-done | bytes 196640 | tf_op jit(solution)/shard_map/ppermute | solution.py:113
  88.7 1.5 %collective-permute-start.9 = (bf16[192,1024]{1,0:T(8,128)(2,1)S(1)}, bf16[192,1024]{1,0:T(8,128)(2,1)S(1)}, u32[]{:S(2)}, u32[]{:S(2)}) collective-permute-start(bf16[192,1024]{1,0:T(8,128)(2,1)S(1)} %bitcast.135), channel_id=1, source_target_pairs={{0,16},{16,0},{1,17},{17,1},{2,18},{18,2},{3,19},{19,3},{4,20},{20... | collective-permute-start | bytes 1179656 | tf_op jit(solution)/shard_map/ppermute | solution.py:77
  90.2 1.2 %fusion = bf16[1,4,64,1024]{3,2,1,0:T(8,128)(2,1)S(1)} fusion(bf16[4,64,768]{2,1,0:T(8,128)(2,1)S(1)} %bitcast.127, bf16[4,768,1024]{2,1,0:T(8,128)(2,1)S(1)} %bitcast.117), kind=kOutput, calls=%fused_computation.2 | convolution fusion | flops 402915328 | bytes 7208960 | tf_op jit(solution)/shard_map/erf,efd->erd/dot_general | solution.py:117
  91.5 1.2 %copy.58 = bf16[1,4,64,1024]{3,1,0,2:T(4,128)(2,1)} copy(bf16[1,4,64,1024]{3,2,1,0:T(8,128)(2,1)S(1)} %fusion) | data formatting | bytes 1048576 | tf_op jit(solution)/shard_map/reshape | solution.py:118
  92.7 5.7 %all-to-all-start.1 = ((bf16[1,4,64,1024]{3,1,0,2:T(4,128)(2,1)}), bf16[1,4,64,1024]{3,1,0,2:T(4,128)(2,1)S(1)}, u32[]{:S(2)}, u32[]{:S(2)}) async-start(bf16[1,4,64,1024]{3,1,0,2:T(4,128)(2,1)} %copy.58), calls=%async_computation.1 | async-start | bytes 1048576 | tf_op jit(solution)/shard_map/all_to_all | solution.py:119
  98.4 0.8 bitcast_dynamic-update-slice_fusion.4
  99.2 0.8 bitcast_dynamic-update-slice_fusion.3
  100.0 0.8 bitcast_dynamic-update-slice_fusion.2
  100.7 0.0 collective-permute-done.8
  100.7 0.8 bitcast_dynamic-update-slice_fusion.1
  101.5 0.0 collective-permute-done.9
  101.5 0.8 bitcast_dynamic-update-slice_fusion
  102.3 10.4 %all-to-all-done.1 = bf16[1,4,64,1024]{3,1,0,2:T(4,128)(2,1)S(1)} async-done(((bf16[1,4,64,1024]{3,1,0,2:T(4,128)(2,1)}), bf16[1,4,64,1024]{3,1,0,2:T(4,128)(2,1)S(1)}, u32[]{:S(2)}, u32[]{:S(2)}) %all-to-all-start.1) | async-done | bytes 524320 | tf_op jit(solution)/shard_map/all_to_all | solution.py:119
  112.7 0.3 copy.64
  112.9 0.1 reshape.130
  113.1 1.0 convolution_convert_fusion.2
  (19 shorter events, 0.2 us)
Async XLA Ops:
  0.6 1.4 %copy-start = (bf16[32,1024]{1,0:T(8,128)(2,1)S(1)}, bf16[32,1024]{1,0:T(8,128)(2,1)}, u32[]{:S(2)}) copy-start(bf16[32,1024]{1,0:T(8,128)(2,1)} %param.7) | copy-start | bytes 196612
  3.4 39.2 %all-to-all-start = ((bf16[16,4,4,1024]{3,2,1,0:T(4,128)(2,1)}), bf16[16,4,4,1024]{3,2,1,0:T(4,128)(2,1)S(1)}, u32[]{:S(2)}, u32[]{:S(2)}) async-start(bf16[16,4,4,1024]{3,2,1,0:T(4,128)(2,1)} %reshape.124), calls=%async_computation | async-start | bytes 1048576 | tf_op jit(solution)/shard_map/all_to_all | solution.py:90
  13.9 27.4 %collective-permute-start.2 = (bf16[192,1024]{1,0:T(8,128)(2,1)}, bf16[192,1024]{1,0:T(8,128)(2,1)S(1)}, u32[]{:S(2)}, u32[]{:S(2)}) collective-permute-start(bf16[192,1024]{1,0:T(8,128)(2,1)} %bitcast.137), channel_id=1, source_target_pairs={{0,16},{16,0},{1,17},{17,1},{2,18},{18,2},{3,19},{19,3},{4,20},{20... | collective-permute-start | bytes 1179656 | tf_op jit(solution)/shard_map/ppermute | solution.py:77
  18.4 32.9 %collective-permute-start.3 = (bf16[192,1024]{1,0:T(8,128)(2,1)}, bf16[192,1024]{1,0:T(8,128)(2,1)S(1)}, u32[]{:S(2)}, u32[]{:S(2)}) collective-permute-start(bf16[192,1024]{1,0:T(8,128)(2,1)} %bitcast.134), channel_id=1, source_target_pairs={{0,16},{16,0},{1,17},{17,1},{2,18},{18,2},{3,19},{19,3},{4,20},{20... | collective-permute-start | bytes 1179656 | tf_op jit(solution)/shard_map/ppermute | solution.py:77
  22.0 31.6 %collective-permute-start.4 = (bf16[192,1024]{1,0:T(8,128)(2,1)}, bf16[192,1024]{1,0:T(8,128)(2,1)S(1)}, u32[]{:S(2)}, u32[]{:S(2)}) collective-permute-start(bf16[192,1024]{1,0:T(8,128)(2,1)} %bitcast.133), channel_id=1, source_target_pairs={{0,16},{16,0},{1,17},{17,1},{2,18},{18,2},{3,19},{19,3},{4,20},{20... | collective-permute-start | bytes 1179656 | tf_op jit(solution)/shard_map/ppermute | solution.py:77
  26.6 71.8 %collective-permute-start.5 = (bf16[192,1024]{1,0:T(8,128)(2,1)}, bf16[192,1024]{1,0:T(8,128)(2,1)S(1)}, u32[]{:S(2)}, u32[]{:S(2)}) collective-permute-start(bf16[192,1024]{1,0:T(8,128)(2,1)} %bitcast.131), channel_id=1, source_target_pairs={{0,16},{16,0},{1,17},{17,1},{2,18},{18,2},{3,19},{19,3},{4,20},{20... | collective-permute-start | bytes 1179656 | tf_op jit(solution)/shard_map/ppermute | solution.py:77
  30.2 69.0 %collective-permute-start.6 = (bf16[192,1024]{1,0:T(8,128)(2,1)}, bf16[192,1024]{1,0:T(8,128)(2,1)S(1)}, u32[]{:S(2)}, u32[]{:S(2)}) collective-permute-start(bf16[192,1024]{1,0:T(8,128)(2,1)} %bitcast.132), channel_id=1, source_target_pairs={{0,16},{16,0},{1,17},{17,1},{2,18},{18,2},{3,19},{19,3},{4,20},{20... | collective-permute-start | bytes 1179656 | tf_op jit(solution)/shard_map/ppermute | solution.py:77
  37.8 3.1 %copy-start.1 = (f32[32,8]{0,1:T(8,128)S(1)}, f32[32,8]{0,1:T(8,128)}, u32[]{:S(2)}) copy-start(f32[32,8]{0,1:T(8,128)} %param.9) | copy-start | bytes 3076
  41.2 58.7 %collective-permute-start.7 = (bf16[192,1024]{1,0:T(8,128)(2,1)}, bf16[192,1024]{1,0:T(8,128)(2,1)S(1)}, u32[]{:S(2)}, u32[]{:S(2)}) collective-permute-start(bf16[192,1024]{1,0:T(8,128)(2,1)} %bitcast.136), channel_id=1, source_target_pairs={{0,16},{16,0},{1,17},{17,1},{2,18},{18,2},{3,19},{19,3},{4,20},{20... | collective-permute-start | bytes 1179656 | tf_op jit(solution)/shard_map/ppermute | solution.py:77
  43.0 47.3 %slice-start = ((s8[6291456]{0:T(1024)(128)(4,1)}), s8[4194304]{0:T(1024)(128)(4,1)S(1)}, s32[]{:S(2)}) async-start(s8[6291456]{0:T(1024)(128)(4,1)} %bitcast.116), calls=%async_computation.2 | async-start | bytes 8388608
  47.1 41.6 %copy-start.2 = (bf16[1,192,1024]{2,1,0:T(8,128)(2,1)S(1)}, bf16[1,192,1024]{2,1,0:T(8,128)(2,1)}, u32[]{:S(2)}) copy-start(bf16[1,192,1024]{2,1,0:T(8,128)(2,1)} %get-tuple-element.33) | copy-start | bytes 1179652
  47.1 43.2 %slice-start.1 = ((s8[6291456]{0:T(1024)(128)(4,1)}), s8[2097152]{0:T(1024)(128)(4,1)S(1)}, s32[]{:S(2)}) async-start(s8[6291456]{0:T(1024)(128)(4,1)} %bitcast.116), calls=%async_computation.3 | async-start | bytes 4194304
  51.3 25.3 %collective-permute-start = (bf16[2,4,32,768]{3,2,1,0:T(8,128)(2,1)S(1)}, bf16[2,4,32,768]{3,2,1,0:T(8,128)(2,1)S(1)}, u32[]{:S(2)}, u32[]{:S(2)}) collective-permute-start(bf16[2,4,32,768]{3,2,1,0:T(8,128)(2,1)S(1)} %pad_maximum_fusion), channel_id=1, source_target_pairs={{0,16},{16,0},{1,17},{17,1},{2,18},{18,2},{3,19},{19,3},{4,20},{20... | collective-permute-start | bytes 1179656 | tf_op jit(solution)/shard_map/ppermute | solution.py:106
  53.6 47.1 %collective-permute-start.8 = (bf16[192,1024]{1,0:T(8,128)(2,1)}, bf16[192,1024]{1,0:T(8,128)(2,1)S(1)}, u32[]{:S(2)}, u32[]{:S(2)}) collective-permute-start(bf16[192,1024]{1,0:T(8,128)(2,1)} %bitcast.35), channel_id=1, source_target_pairs={{0,16},{16,0},{1,17},{17,1},{2,18},{18,2},{3,19},{19,3},{4,20},{20... | collective-permute-start | bytes 1179656 | tf_op jit(solution)/shard_map/ppermute | solution.py:77
  76.8 11.9 %collective-permute-start.1 = (bf16[4,32,768]{2,1,0:T(8,128)(2,1)S(1)}, bf16[4,32,768]{2,1,0:T(8,128)(2,1)S(1)}, u32[]{:S(2)}, u32[]{:S(2)}) collective-permute-start(bf16[4,32,768]{2,1,0:T(8,128)(2,1)S(1)} %fusion.8), channel_id=1, source_target_pairs={{0,16},{16,0},{1,17},{17,1},{2,18},{18,2},{3,19},{19,3},{4,20},{20... | collective-permute-start | bytes 589832 | tf_op jit(solution)/shard_map/ppermute | solution.py:113
  88.7 12.8 %collective-permute-start.9 = (bf16[192,1024]{1,0:T(8,128)(2,1)S(1)}, bf16[192,1024]{1,0:T(8,128)(2,1)S(1)}, u32[]{:S(2)}, u32[]{:S(2)}) collective-permute-start(bf16[192,1024]{1,0:T(8,128)(2,1)S(1)} %bitcast.135), channel_id=1, source_target_pairs={{0,16},{16,0},{1,17},{17,1},{2,18},{18,2},{3,19},{19,3},{4,20},{20... | collective-permute-start | bytes 1179656 | tf_op jit(solution)/shard_map/ppermute | solution.py:77
  92.7 20.0 %all-to-all-start.1 = ((bf16[1,4,64,1024]{3,1,0,2:T(4,128)(2,1)}), bf16[1,4,64,1024]{3,1,0,2:T(4,128)(2,1)S(1)}, u32[]{:S(2)}, u32[]{:S(2)}) async-start(bf16[1,4,64,1024]{3,1,0,2:T(4,128)(2,1)} %copy.58), calls=%async_computation.1 | async-start | bytes 1048576 | tf_op jit(solution)/shard_map/all_to_all | solution.py:119

commit v3 on v2

--- a/solution.py
+++ b/solution.py
@@ -16,21 +16,22 @@
 
 def narrow(where, trained, synced, expert, part, piece, ways, width):
     experts, trained_rows, _ = trained.shape
-    step = 64 if piece % 64 == 0 else piece
+    step = 96 if piece % 96 == 0 else piece
     steps = piece // step
 
-    def body(where_ref, strip_ref, *refs):
+    def body(where_ref, *refs):
         sent_ref, own_ref = refs[-2:]
-        for s in range(ways):
-            owner = lax.rem(where_ref[0] + s, ways)
-            columns = strip_ref[0, :, pl.ds(pl.multiple_of(owner * width, 128), width)]
-            if s:
-                sent_ref[s - 1] = columns.astype(jnp.bfloat16)
-            else:
-                own_ref[0, 0] = columns.astype(jnp.bfloat16)
+        own_ref[0, 0] = refs[0][0].astype(jnp.bfloat16)
+        for s in range(1, ways):
+            sent_ref[s - 1] = refs[s][0].astype(jnp.bfloat16)
 
-    in_specs = [pl.BlockSpec((1, step, ways * width), lambda i, w: (expert, part * steps + i, 0))]
-    operands = [where, trained]
+    def columns(s):
+        return pl.BlockSpec(
+            (1, step, width), lambda i, w: (expert, part * steps + i, lax.rem(w[0] + s, ways))
+        )
+
+    in_specs = [columns(s) for s in range(ways)]
+    operands = [where] + [trained] * ways
     if synced is not None:
         in_specs.append(pl.BlockSpec(memory_space=pl.ANY))
         operands.append(synced)
@@ -49,7 +50,7 @@
             jax.ShapeDtypeStruct((ways - 1, piece, width), jnp.bfloat16),
             jax.ShapeDtypeStruct((experts, ways, trained_rows, width), jnp.bfloat16),
         ],
-        input_output_aliases={} if synced is None else {2: 1},
+        input_output_aliases={} if synced is None else {ways + 1: 1},
     )(*operands)
 
 
@@ -107,6 +108,7 @@
         gate_sum = gate_sum + pair[0].astype(jnp.float32)
         up_sum = up_sum + pair[1].astype(jnp.float32)
     hidden_own = (jax.nn.silu(gate_sum) * up_sum).astype(jnp.bfloat16)
+    synced, hidden_own = lax.optimization_barrier((synced, hidden_own))
     hidden = jnp.zeros((expert_local, ways, share, hid), jnp.bfloat16)
     hidden = lax.dynamic_update_index_in_dim(hidden, hidden_own, me, 1)
     for s in range(1, ways):

time: 115 us -> 134 us (1.17)
  waiting for transfers between devices: 42.3 us -> 65.1 us
  Pallas kernels: 24.5 us -> 17.3 us
  local copies, waits for them, and re-layouts: 10.5 us -> 13.4 us
    ppermute x1, waiting for transfers between devices: 10.2 us -> 34.8 us  [local(): other = lax.ppermute(hidden_own, 'dp', ring(ways, s))]
    ppermute x1, waiting for transfers between devices: 21.7 us -> 0.01 us  [local(): pair = lax.ppermute(pair, 'dp', ring(ways, s))]
    all_to_all x1, waiting for transfers between devices: 0.01 us -> 14.3 us  [local(): lax.all_to_all(outgoing, 'expert', split_axis=0, concat_axis=2, tiled=True)]
    pallas_call x8, Pallas kernels: 24.5 us -> 17.3 us  [narrow(): pl.pallas_call(body, grid_spec=pltpu.PrefetchScalarGridSpec(num_scalar_pr...]
    ppermute x8, waiting for transfers between devices: 0.02 us -> 5.72 us  [local(): lax.ppermute(sent[s - 1], 'dp', ring(ways, s))]
    dot_general x1, matrix products: 4.1 us -> 1.17 us  [local(): jnp.einsum('erd,edf->erf', arrived, up_weight, preferred_element_type=jnp...]
    dot_general x1, matrix products: 1.21 us -> 4.03 us  [local(): jnp.einsum('erf,efd->erd', hidden, down_weight, preferred_element_type=jn...]
    dynamic_update_slice x8, local copies, waits for them, and re-layouts: 6.18 us -> 8.17 us  [local(): lax.dynamic_update_slice(synced, arrival[None, None], (expert, (me - s) %...]
  transfers between devices with their start and end apart: 12 -> 12, of which waited for: 3 -> 5; matrix products, arithmetic and copies ran while one was open for 16% -> 11% of each run, Pallas kernels for 21% -> 13%
where the time goes in v3:
time: 134 us; the launch traced here: 133 us
  waiting for transfers between devices  65.1 us (49%)
  starting transfers between devices  24 us (18%)
  Pallas kernels  17.3 us (13%)
  local copies, waits for them, and re-layouts  13.4 us (10%)
  matrix products  10.7 us (8%)
  other arithmetic  1.59 us (1%)
    ppermute x1, waiting for transfers between devices, local(): other = lax.ppermute(hidden_own, 'dp', ring(ways, s))  34.8 us
    pallas_call x8, Pallas kernels, narrow(): pl.pallas_call(body, grid_spec=pltpu.PrefetchScalarGridSpec(num_scalar_pr...  17.3 us
    all_to_all x1, waiting for transfers between devices, local(): lax.all_to_all(outgoing, 'expert', split_axis=0, concat_axis=2, tiled=True)  14.3 us
    all_to_all x1, waiting for transfers between devices, local(): lax.all_to_all(expert_out, 'expert', split_axis=2, concat_axis=0, tiled=T...  10.4 us
    ppermute x8, starting transfers between devices, local(): lax.ppermute(sent[s - 1], 'dp', ring(ways, s))  9.18 us
    dynamic_update_slice x8, local copies, waits for them, and re-layouts, local(): lax.dynamic_update_slice(synced, arrival[None, None], (expert, (me - s) %...  8.17 us
    all_to_all x1, starting transfers between devices, local(): lax.all_to_all(outgoing, 'expert', split_axis=0, concat_axis=2, tiled=True)  7.41 us
    ppermute x8, waiting for transfers between devices, local(): lax.ppermute(sent[s - 1], 'dp', ring(ways, s))  5.72 us
  transfers between devices with their start and end apart: 12, of which 5 were waited for; matrix products, arithmetic and copies ran while one was open for 11% of the time, Pallas kernels for 13%

profile of v3, /device:TPU:0, one launch (start us, length us, event | category | flops | bytes accessed | tf_op | source)
XLA Modules:
  0.0 133.0 jit_solution(8680537902767047420)
XLA Ops:
  0.6 0.0 copy-start
  0.6 0.8 copy.41
  1.4 0.1 convert_reduce_fusion
  1.6 0.1 reduce_window_sum.11
  1.6 0.1 copy.43
  1.7 0.1 copy.42
  1.8 0.1 eq.77
  2.0 0.0 slice-start
  2.0 0.3 convolution_convert_fusion.1
  2.4 1.0 reshape.101
  3.4 7.4 %all-to-all-start = ((bf16[16,4,4,1024]{3,2,1,0:T(4,128)(2,1)}), bf16[16,4,4,1024]{3,2,1,0:T(4,128)(2,1)S(1)}, u32[]{:S(2)}, u32[]{:S(2)}) async-start(bf16[16,4,4,1024]{3,2,1,0:T(4,128)(2,1)} %reshape.101), calls=%async_computation | async-start | bytes 1048576 | tf_op jit(solution)/shard_map/all_to_all | solution.py:91
  10.8 14.3 %all-to-all-done = bf16[16,4,4,1024]{3,2,1,0:T(4,128)(2,1)S(1)} async-done(((bf16[16,4,4,1024]{3,2,1,0:T(4,128)(2,1)}), bf16[16,4,4,1024]{3,2,1,0:T(4,128)(2,1)S(1)}, u32[]{:S(2)}, u32[]{:S(2)}) %all-to-all-start) | async-done | bytes 524320 | tf_op jit(solution)/shard_map/all_to_all | solution.py:91
  25.1 0.2 copy.46
  25.3 0.1 reshape.102
  25.4 0.0 slice-start.1
  25.4 4.1 %fusion.10 = f32[4,64,768]{2,1,0:T(8,128)S(1)} fusion(bf16[4,64,1024]{2,1,0:T(8,128)(2,1)S(1)} %reshape.102, bf16[4,1024,768]{2,1,0:T(8,128)(2,1)} %param.10), kind=kOutput, calls=%fused_computation.36 | convolution fusion | flops 402653184 | bytes 7602176 | tf_op jit(solution)/shard_map/erd,edf->erf/dot_general | solution.py:94
  29.5 1.2 fusion.11
  30.7 0.9 copy-done.1
  31.7 1.6 %collective-permute-start = (bf16[2,4,32,768]{3,2,1,0:T(8,128)(2,1)S(1)}, bf16[2,4,32,768]{3,2,1,0:T(8,128)(2,1)}, u32[]{:S(2)}, u32[]{:S(2)}) collective-permute-start(bf16[2,4,32,768]{3,2,1,0:T(8,128)(2,1)S(1)} %pad_maximum_fusion), channel_id=1, source_target_pairs={{0,16},{16,0},{1,17},{17,1},{2,18},{18,2},{3,19},{19,3},{4,20},{20... | collective-permute-start | bytes 1179656 | tf_op jit(solution)/shard_map/ppermute | solution.py:107
  33.2 2.1 %shard_map.86 = (bf16[1,192,1024]{2,1,0:T(8,128)(2,1)}, bf16[4,2,384,1024]{3,2,1,0:T(8,128)(2,1)}) custom-call(s32[1]{0:T(128)} %bitcast.1.where_ref, f32[4,384,2048]{2,1,0:T(8,128)} %refs_1_.15, f32[4,384,2048]{2,1,0:T(8,128)} %refs_1_.15), custom_call_target="tpu_custom_call" | custom-call | tf_op jit(solution)/shard_map/pallas_call | solution.py:38
  35.4 0.5 collective-permute-start.2
  35.9 2.1 %shard_map.87 = (bf16[1,192,1024]{2,1,0:T(8,128)(2,1)}, bf16[4,2,384,1024]{3,2,1,0:T(8,128)(2,1)}) custom-call(s32[1]{0:T(128)} %bitcast.1.where_ref, f32[4,384,2048]{2,1,0:T(8,128)} %refs_1_.15, f32[4,384,2048]{2,1,0:T(8,128)} %refs_1_.15, bf16[4,2,384,1024]{3,2,1,0:T(8,128)(2,1)} %get-tuple-element.20.refs_2_), custom_call_target="tpu_custom_call", output_to_operand_aliasing={{1}: (3, {})} | custom-call | tf_op jit(solution)/shard_map/pallas_call | solution.py:38
  38.0 1.5 %collective-permute-start.3 = (bf16[192,1024]{1,0:T(8,128)(2,1)}, bf16[192,1024]{1,0:T(8,128)(2,1)}, u32[]{:S(2)}, u32[]{:S(2)}) collective-permute-start(bf16[192,1024]{1,0:T(8,128)(2,1)} %bitcast.103), channel_id=1, source_target_pairs={{0,16},{16,0},{1,17},{17,1},{2,18},{18,2},{3,19},{19,3},{4,20},{20... | collective-permute-start | bytes 1179656 | tf_op jit(solution)/shard_map/ppermute | solution.py:78
  39.5 2.1 %shard_map.88 = (bf16[1,192,1024]{2,1,0:T(8,128)(2,1)}, bf16[4,2,384,1024]{3,2,1,0:T(8,128)(2,1)}) custom-call(s32[1]{0:T(128)} %bitcast.1.where_ref, f32[4,384,2048]{2,1,0:T(8,128)} %refs_1_.15, f32[4,384,2048]{2,1,0:T(8,128)} %refs_1_.15, bf16[4,2,384,1024]{3,2,1,0:T(8,128)(2,1)} %get-tuple-element.21.refs_2_), custom_call_target="tpu_custom_call", output_to_operand_aliasing={{1}: (3, {})} | custom-call | tf_op jit(solution)/shard_map/pallas_call | solution.py:38
  41.7 0.5 collective-permute-start.4
  42.2 2.1 %shard_map.89 = (bf16[1,192,1024]{2,1,0:T(8,128)(2,1)}, bf16[4,2,384,1024]{3,2,1,0:T(8,128)(2,1)}) custom-call(s32[1]{0:T(128)} %bitcast.1.where_ref, f32[4,384,2048]{2,1,0:T(8,128)} %refs_1_.15, f32[4,384,2048]{2,1,0:T(8,128)} %refs_1_.15, bf16[4,2,384,1024]{3,2,1,0:T(8,128)(2,1)} %get-tuple-element.22.refs_2_), custom_call_target="tpu_custom_call", output_to_operand_aliasing={{1}: (3, {})} | custom-call | tf_op jit(solution)/shard_map/pallas_call | solution.py:38
  44.4 1.5 %collective-permute-start.5 = (bf16[192,1024]{1,0:T(8,128)(2,1)}, bf16[192,1024]{1,0:T(8,128)(2,1)S(1)}, u32[]{:S(2)}, u32[]{:S(2)}) collective-permute-start(bf16[192,1024]{1,0:T(8,128)(2,1)} %bitcast.98), channel_id=1, source_target_pairs={{0,16},{16,0},{1,17},{17,1},{2,18},{18,2},{3,19},{19,3},{4,20},{20... | collective-permute-start | bytes 1179656 | tf_op jit(solution)/shard_map/ppermute | solution.py:78
  45.9 2.1 %shard_map.90 = (bf16[1,192,1024]{2,1,0:T(8,128)(2,1)}, bf16[4,2,384,1024]{3,2,1,0:T(8,128)(2,1)}) custom-call(s32[1]{0:T(128)} %bitcast.1.where_ref, f32[4,384,2048]{2,1,0:T(8,128)} %refs_1_.15, f32[4,384,2048]{2,1,0:T(8,128)} %refs_1_.15, bf16[4,2,384,1024]{3,2,1,0:T(8,128)(2,1)} %get-tuple-element.23.refs_2_), custom_call_target="tpu_custom_call", output_to_operand_aliasing={{1}: (3, {})} | custom-call | tf_op jit(solution)/shard_map/pallas_call | solution.py:38
  48.0 2.2 %shard_map.91 = (bf16[1,192,1024]{2,1,0:T(8,128)(2,1)}, bf16[4,2,384,1024]{3,2,1,0:T(8,128)(2,1)}) custom-call(s32[1]{0:T(128)} %bitcast.1.where_ref, f32[4,384,2048]{2,1,0:T(8,128)} %refs_1_.15, f32[4,384,2048]{2,1,0:T(8,128)} %refs_1_.15, bf16[4,2,384,1024]{3,2,1,0:T(8,128)(2,1)} %get-tuple-element.24.refs_2_), custom_call_target="tpu_custom_call", output_to_operand_aliasing={{1}: (3, {})} | custom-call | tf_op jit(solution)/shard_map/pallas_call | solution.py:38
  50.1 2.2 %shard_map.92 = (bf16[1,192,1024]{2,1,0:T(8,128)(2,1)}, bf16[4,2,384,1024]{3,2,1,0:T(8,128)(2,1)}) custom-call(s32[1]{0:T(128)} %bitcast.1.where_ref, f32[4,384,2048]{2,1,0:T(8,128)} %refs_1_.15, f32[4,384,2048]{2,1,0:T(8,128)} %refs_1_.15, bf16[4,2,384,1024]{3,2,1,0:T(8,128)(2,1)} %get-tuple-element.25.refs_2_), custom_call_target="tpu_custom_call", output_to_operand_aliasing={{1}: (3, {})} | custom-call | tf_op jit(solution)/shard_map/pallas_call | solution.py:38
  52.3 2.2 %shard_map.93 = (bf16[1,192,1024]{2,1,0:T(8,128)(2,1)}, bf16[4,2,384,1024]{3,2,1,0:T(8,128)(2,1)}) custom-call(s32[1]{0:T(128)} %bitcast.1.where_ref, f32[4,384,2048]{2,1,0:T(8,128)} %refs_1_.15, f32[4,384,2048]{2,1,0:T(8,128)} %refs_1_.15, bf16[4,2,384,1024]{3,2,1,0:T(8,128)(2,1)} %get-tuple-element.26.refs_2_), custom_call_target="tpu_custom_call", output_to_operand_aliasing={{1}: (3, {})} | custom-call | tf_op jit(solution)/shard_map/pallas_call | solution.py:38
  54.6 0.1 copy.44
  54.7 0.1 select_reduce_fusion
  54.8 0.1 copy.45
  54.9 0.1 fusion.6
  55.0 0.0 collective-permute-done
  55.0 0.6 collective-permute-start.6
  55.6 1.2 fusion.2
  56.7 0.0 collective-permute-done.2
  56.8 1.6 %collective-permute-start.7 = (bf16[192,1024]{1,0:T(8,128)(2,1)}, bf16[192,1024]{1,0:T(8,128)(2,1)S(1)}, u32[]{:S(2)}, u32[]{:S(2)}) collective-permute-start(bf16[192,1024]{1,0:T(8,128)(2,1)} %bitcast.102), channel_id=1, source_target_pairs={{0,16},{16,0},{1,17},{17,1},{2,18},{18,2},{3,19},{19,3},{4,20},{20... | collective-permute-start | bytes 1179656 | tf_op jit(solution)/shard_map/ppermute | solution.py:78
  58.3 1.8 %bitcast_dynamic-update-slice_fusion.7 = bf16[4,2,384,1024]{3,2,1,0:T(8,128)(2,1)} fusion(bf16[4,2,384,1024]{3,2,1,0:T(8,128)(2,1)} %get-tuple-element.29, s32[]{:T(128)S(6)} %select_n.58, bf16[192,1024]{1,0:T(8,128)(2,1)} %collective-permute-done.2), kind=kLoop, calls=%fused_computation.18 | loop fusion | bytes 786436 | tf_op jit(solution)/shard_map/dynamic_update_slice | solution.py:137
  60.1 0.6 collective-permute-done.3
  60.7 1.5 %collective-permute-start.8 = (bf16[192,1024]{1,0:T(8,128)(2,1)}, bf16[192,1024]{1,0:T(8,128)(2,1)S(1)}, u32[]{:S(2)}, u32[]{:S(2)}) collective-permute-start(bf16[192,1024]{1,0:T(8,128)(2,1)} %bitcast.100), channel_id=1, source_target_pairs={{0,16},{16,0},{1,17},{17,1},{2,18},{18,2},{3,19},{19,3},{4,20},{20... | collective-permute-start | bytes 1179656 | tf_op jit(solution)/shard_map/ppermute | solution.py:78
  62.2 1.8 %bitcast_dynamic-update-slice_fusion.6 = bf16[4,2,384,1024]{3,2,1,0:T(8,128)(2,1)} fusion(bf16[4,2,384,1024]{3,2,1,0:T(8,128)(2,1)} %bitcast_dynamic-update-slice_fusion.7, s32[]{:T(128)S(6)} %select_n.58, bf16[192,1024]{1,0:T(8,128)(2,1)} %collective-permute-done.3), kind=kLoop, calls=%fused_computation.17 | loop fusion | bytes 786436 | tf_op jit(solution)/shard_map/dynamic_update_slice | solution.py:137
  64.0 5.1 %collective-permute-done.4 = bf16[192,1024]{1,0:T(8,128)(2,1)S(1)} collective-permute-done((bf16[192,1024]{1,0:T(8,128)(2,1)}, bf16[192,1024]{1,0:T(8,128)(2,1)S(1)}, u32[]{:S(2)}, u32[]{:S(2)}) %collective-permute-start.4) | collective-permute-done | bytes 393248 | tf_op jit(solution)/shard_map/ppermute | solution.py:78
  69.0 1.5 %collective-permute-start.1 = (bf16[4,32,768]{2,1,0:T(8,128)(2,1)S(1)}, bf16[4,32,768]{2,1,0:T(8,128)(2,1)S(1)}, u32[]{:S(2)}, u32[]{:S(2)}) collective-permute-start(bf16[4,32,768]{2,1,0:T(8,128)(2,1)S(1)} %fusion.2), channel_id=1, source_target_pairs={{0,16},{16,0},{1,17},{17,1},{2,18},{18,2},{3,19},{19,3},{4,20},{20... | collective-permute-start | bytes 589832 | tf_op jit(solution)/shard_map/ppermute | solution.py:115
  70.5 0.8 bitcast_dynamic-update-slice_fusion.5
  71.3 34.8 %collective-permute-done.1 = bf16[4,32,768]{2,1,0:T(8,128)(2,1)S(1)} collective-permute-done((bf16[4,32,768]{2,1,0:T(8,128)(2,1)S(1)}, bf16[4,32,768]{2,1,0:T(8,128)(2,1)S(1)}, u32[]{:S(2)}, u32[]{:S(2)}) %collective-permute-start.1) | collective-permute-done | bytes 196640 | tf_op jit(solution)/shard_map/ppermute | solution.py:115
  106.1 1.5 %collective-permute-start.9 = (bf16[192,1024]{1,0:T(8,128)(2,1)}, bf16[192,1024]{1,0:T(8,128)(2,1)S(1)}, u32[]{:S(2)}, u32[]{:S(2)}) collective-permute-start(bf16[192,1024]{1,0:T(8,128)(2,1)} %bitcast.99), channel_id=1, source_target_pairs={{0,16},{16,0},{1,17},{17,1},{2,18},{18,2},{3,19},{19,3},{4,20},{20... | collective-permute-start | bytes 1179656 | tf_op jit(solution)/shard_map/ppermute | solution.py:78
  107.6 4.0 %fusion = bf16[1,4,64,1024]{3,2,1,0:T(8,128)(2,1)S(1)} fusion(bf16[4,64,768]{2,1,0:T(8,128)(2,1)S(1)} %bitcast.94, bf16[4,768,1024]{2,1,0:T(8,128)(2,1)} %param.12), kind=kOutput, calls=%fused_computation.2 | convolution fusion | flops 402915328 | bytes 7208960 | tf_op jit(solution)/shard_map/erf,efd->erd/dot_general | solution.py:119
  111.7 1.2 copy.50
  112.9 4.4 %all-to-all-start.1 = ((bf16[1,4,64,1024]{3,1,0,2:T(4,128)(2,1)}), bf16[1,4,64,1024]{3,1,0,2:T(4,128)(2,1)S(1)}, u32[]{:S(2)}, u32[]{:S(2)}) async-start(bf16[1,4,64,1024]{3,1,0,2:T(4,128)(2,1)} %copy.50), calls=%async_computation.1 | async-start | bytes 1048576 | tf_op jit(solution)/shard_map/all_to_all | solution.py:121
  117.3 0.0 collective-permute-done.5
  117.3 0.8 bitcast_dynamic-update-slice_fusion.4
  118.1 0.0 collective-permute-done.6
  118.1 0.8 bitcast_dynamic-update-slice_fusion.3
  118.9 0.0 collective-permute-done.7
  118.9 0.8 bitcast_dynamic-update-slice_fusion.2
  119.7 0.8 bitcast_dynamic-update-slice_fusion.1
  120.4 0.8 bitcast_dynamic-update-slice_fusion
  121.2 10.4 %all-to-all-done.1 = bf16[1,4,64,1024]{3,1,0,2:T(4,128)(2,1)S(1)} async-done(((bf16[1,4,64,1024]{3,1,0,2:T(4,128)(2,1)}), bf16[1,4,64,1024]{3,1,0,2:T(4,128)(2,1)S(1)}, u32[]{:S(2)}, u32[]{:S(2)}) %all-to-all-start.1) | async-done | bytes 524320 | tf_op jit(solution)/shard_map/all_to_all | solution.py:121
  131.6 0.3 copy.54
  131.9 0.1 reshape.107
  132.0 1.0 convolution_convert_fusion.2
  (21 shorter events, 0.3 us)
Async XLA Ops:
  0.6 1.4 %copy-start = (bf16[32,1024]{1,0:T(8,128)(2,1)S(1)}, bf16[32,1024]{1,0:T(8,128)(2,1)}, u32[]{:S(2)}) copy-start(bf16[32,1024]{1,0:T(8,128)(2,1)} %param.7) | copy-start | bytes 196612
  2.0 27.5 %slice-start = ((s8[6291456]{0:T(1024)(128)(4,1)}), s8[2097152]{0:T(1024)(128)(4,1)S(1)}, s32[]{:S(2)}) async-start(s8[6291456]{0:T(1024)(128)(4,1)} %bitcast.85), calls=%async_computation.2 | async-start | bytes 4194304
  3.4 21.7 %all-to-all-start = ((bf16[16,4,4,1024]{3,2,1,0:T(4,128)(2,1)}), bf16[16,4,4,1024]{3,2,1,0:T(4,128)(2,1)S(1)}, u32[]{:S(2)}, u32[]{:S(2)}) async-start(bf16[16,4,4,1024]{3,2,1,0:T(4,128)(2,1)} %reshape.101), calls=%async_computation | async-start | bytes 1048576 | tf_op jit(solution)/shard_map/all_to_all | solution.py:91
  25.4 4.1 %slice-start.1 = ((s8[6291456]{0:T(1024)(128)(4,1)}), s8[4194304]{0:T(1024)(128)(4,1)S(1)}, s32[]{:S(2)}) async-start(s8[6291456]{0:T(1024)(128)(4,1)} %bitcast.85), calls=%async_computation.3 | async-start | bytes 8388608
  30.7 0.9 copy-start.1
  31.7 23.3 %collective-permute-start = (bf16[2,4,32,768]{3,2,1,0:T(8,128)(2,1)S(1)}, bf16[2,4,32,768]{3,2,1,0:T(8,128)(2,1)}, u32[]{:S(2)}, u32[]{:S(2)}) collective-permute-start(bf16[2,4,32,768]{3,2,1,0:T(8,128)(2,1)S(1)} %pad_maximum_fusion), channel_id=1, source_target_pairs={{0,16},{16,0},{1,17},{17,1},{2,18},{18,2},{3,19},{19,3},{4,20},{20... | collective-permute-start | bytes 1179656 | tf_op jit(solution)/shard_map/ppermute | solution.py:107
  35.4 21.4 %collective-permute-start.2 = (bf16[192,1024]{1,0:T(8,128)(2,1)}, bf16[192,1024]{1,0:T(8,128)(2,1)}, u32[]{:S(2)}, u32[]{:S(2)}) collective-permute-start(bf16[192,1024]{1,0:T(8,128)(2,1)} %bitcast.105), channel_id=1, source_target_pairs={{0,16},{16,0},{1,17},{17,1},{2,18},{18,2},{3,19},{19,3},{4,20},{20... | collective-permute-start | bytes 1179656 | tf_op jit(solution)/shard_map/ppermute | solution.py:78
  38.0 22.7 %collective-permute-start.3 = (bf16[192,1024]{1,0:T(8,128)(2,1)}, bf16[192,1024]{1,0:T(8,128)(2,1)}, u32[]{:S(2)}, u32[]{:S(2)}) collective-permute-start(bf16[192,1024]{1,0:T(8,128)(2,1)} %bitcast.103), channel_id=1, source_target_pairs={{0,16},{16,0},{1,17},{17,1},{2,18},{18,2},{3,19},{19,3},{4,20},{20... | collective-permute-start | bytes 1179656 | tf_op jit(solution)/shard_map/ppermute | solution.py:78
  41.7 27.4 %collective-permute-start.4 = (bf16[192,1024]{1,0:T(8,128)(2,1)}, bf16[192,1024]{1,0:T(8,128)(2,1)S(1)}, u32[]{:S(2)}, u32[]{:S(2)}) collective-permute-start(bf16[192,1024]{1,0:T(8,128)(2,1)} %bitcast.101), channel_id=1, source_target_pairs={{0,16},{16,0},{1,17},{17,1},{2,18},{18,2},{3,19},{19,3},{4,20},{20... | collective-permute-start | bytes 1179656 | tf_op jit(solution)/shard_map/ppermute | solution.py:78
  44.4 73.0 %collective-permute-start.5 = (bf16[192,1024]{1,0:T(8,128)(2,1)}, bf16[192,1024]{1,0:T(8,128)(2,1)S(1)}, u32[]{:S(2)}, u32[]{:S(2)}) collective-permute-start(bf16[192,1024]{1,0:T(8,128)(2,1)} %bitcast.98), channel_id=1, source_target_pairs={{0,16},{16,0},{1,17},{17,1},{2,18},{18,2},{3,19},{19,3},{4,20},{20... | collective-permute-start | bytes 1179656 | tf_op jit(solution)/shard_map/ppermute | solution.py:78
  52.3 2.3 %copy-start.3 = (f32[32,8]{0,1:T(8,128)S(1)}, f32[32,8]{0,1:T(8,128)}, u32[]{:S(2)}) copy-start(f32[32,8]{0,1:T(8,128)} %param.9) | copy-start | bytes 3076
  52.3 3.3 %copy-start.2 = (f32[4,64,768]{2,1,0:T(8,128)S(1)}, f32[4,64,768]{2,1,0:T(8,128)}, u32[]{:S(2)}) copy-start(f32[4,64,768]{2,1,0:T(8,128)} %copy-done.1) | copy-start | bytes 2359300
  55.0 63.1 %collective-permute-start.6 = (bf16[192,1024]{1,0:T(8,128)(2,1)}, bf16[192,1024]{1,0:T(8,128)(2,1)S(1)}, u32[]{:S(2)}, u32[]{:S(2)}) collective-permute-start(bf16[192,1024]{1,0:T(8,128)(2,1)} %bitcast.104), channel_id=1, source_target_pairs={{0,16},{16,0},{1,17},{17,1},{2,18},{18,2},{3,19},{19,3},{4,20},{20... | collective-permute-start | bytes 1179656 | tf_op jit(solution)/shard_map/ppermute | solution.py:78
  56.8 62.1 %collective-permute-start.7 = (bf16[192,1024]{1,0:T(8,128)(2,1)}, bf16[192,1024]{1,0:T(8,128)(2,1)S(1)}, u32[]{:S(2)}, u32[]{:S(2)}) collective-permute-start(bf16[192,1024]{1,0:T(8,128)(2,1)} %bitcast.102), channel_id=1, source_target_pairs={{0,16},{16,0},{1,17},{17,1},{2,18},{18,2},{3,19},{19,3},{4,20},{20... | collective-permute-start | bytes 1179656 | tf_op jit(solution)/shard_map/ppermute | solution.py:78
  60.7 58.9 %collective-permute-start.8 = (bf16[192,1024]{1,0:T(8,128)(2,1)}, bf16[192,1024]{1,0:T(8,128)(2,1)S(1)}, u32[]{:S(2)}, u32[]{:S(2)}) collective-permute-start(bf16[192,1024]{1,0:T(8,128)(2,1)} %bitcast.100), channel_id=1, source_target_pairs={{0,16},{16,0},{1,17},{17,1},{2,18},{18,2},{3,19},{19,3},{4,20},{20... | collective-permute-start | bytes 1179656 | tf_op jit(solution)/shard_map/ppermute | solution.py:78
  69.0 37.1 %collective-permute-start.1 = (bf16[4,32,768]{2,1,0:T(8,128)(2,1)S(1)}, bf16[4,32,768]{2,1,0:T(8,128)(2,1)S(1)}, u32[]{:S(2)}, u32[]{:S(2)}) collective-permute-start(bf16[4,32,768]{2,1,0:T(8,128)(2,1)S(1)} %fusion.2), channel_id=1, source_target_pairs={{0,16},{16,0},{1,17},{17,1},{2,18},{18,2},{3,19},{19,3},{4,20},{20... | collective-permute-start | bytes 589832 | tf_op jit(solution)/shard_map/ppermute | solution.py:115
  106.1 14.3 %collective-permute-start.9 = (bf16[192,1024]{1,0:T(8,128)(2,1)}, bf16[192,1024]{1,0:T(8,128)(2,1)S(1)}, u32[]{:S(2)}, u32[]{:S(2)}) collective-permute-start(bf16[192,1024]{1,0:T(8,128)(2,1)} %bitcast.99), channel_id=1, source_target_pairs={{0,16},{16,0},{1,17},{17,1},{2,18},{18,2},{3,19},{19,3},{4,20},{20... | collective-permute-start | bytes 1179656 | tf_op jit(solution)/shard_map/ppermute | solution.py:78
  112.9 18.7 %all-to-all-start.1 = ((bf16[1,4,64,1024]{3,1,0,2:T(4,128)(2,1)}), bf16[1,4,64,1024]{3,1,0,2:T(4,128)(2,1)S(1)}, u32[]{:S(2)}, u32[]{:S(2)}) async-start(bf16[1,4,64,1024]{3,1,0,2:T(4,128)(2,1)} %copy.50), calls=%async_computation.1 | async-start | bytes 1048576 | tf_op jit(solution)/shard_map/all_to_all | solution.py:121
